TPU v7x, 32 devices: a whole 2x2x4 slice. The times are simulated.
32 devices in a mesh: qrow: 8 (over y, x, core), kcol: 4 (over z).
Axes of the slice: x: 2, y: 2, z: 4, core: 2. Of those that a mesh axis runs over, the one named last changes fastest.
Arguments:
- query_states: bfloat16 [32768, 512], P(('qrow', 'kcol')), may hold values from -8 to 8
- key_states: bfloat16 [32768, 512], P(('kcol', 'qrow')), may hold values from -8 to 8
- value_states: bfloat16 [32768, 512], P(('kcol', 'qrow')), may hold values from -6 to 6
- saved_output: bfloat16 [32768, 512], P(('qrow', 'kcol')), may hold values from -0.59765625 to 0.59765625
- output_grad: bfloat16 [32768, 512], P(('qrow', 'kcol')), may hold values from -6 to 6
- normalizer: float32 [32768, 4], P(('qrow', 'kcol')), as said below
- doc_lengths: int32 [8], replicated, may hold values from 1 to 8192, as said below
Outputs:
- query_grad: bfloat16 [32768, 512], P(('qrow', 'kcol'))
- key_grad: bfloat16 [32768, 512], P(('kcol', 'qrow'))
- value_grad: bfloat16 [32768, 512], P(('kcol', 'qrow'))
Inputs may be any that keep to these rules, and one draw needn't show every extreme that they name: `doc_lengths`: the 8 lengths sum to 32768; exactly one of them equals 8192, every other one is smaller. normalizer[p, h] is the logarithm of the sum of exp(scores[h, p, t]) over the t that allowed admits, computed in float32 from query_states, key_states and doc_lengths.
All inputs are finite; a program needn't handle non-finite values.
Results may differ from a plain program's by a relative error of at most 0.005.
Values may be sent and summed in bfloat16 or wider, within the bound.
A program may use at most 704 MiB of HBM per device.

v0:
```python
import functools
import math

import jax
import jax.numpy as jnp
from jax import lax
from jax.experimental import pallas as pl
from jax.experimental.pallas import tpu as pltpu
from jax.sharding import Mesh, PartitionSpec as P

HEAD_DIM = 128
KV_HEADS = 4
TILE_Q = 512
TILE_K = 256
SCALING = HEAD_DIM ** (-0.5)
LOG2E = math.log2(math.e)

Q_AXES = ("yx", "core", "ko", "head")
K_AXES = ("ko", "head", "yx", "core")


def dot(a, b, dims):
    return lax.dot_general(a, b, (dims, ((), ())), preferred_element_type=jnp.float32)


def attention_kernel(
    piece, groups, docs, ends_ref, where_ref, q_ref, g_ref, nd_ref, k_ref, v_ref,
    dq_ref, dk_ref, dv_ref, dq_acc, dk_acc, dv_acc,
):
    tile_q = nd_ref.shape[2]
    tile_k = dk_acc.shape[0]
    q_tiles = q_ref.shape[0] // tile_q
    k_tiles = k_ref.shape[0] // tile_k
    core = where_ref[0]
    group = where_ref[1]
    run = 2 * piece

    def key_token(i):
        return (i // run) * (groups * run) + group * run + i % run

    def doc_end(position):
        end = jnp.zeros_like(position)
        for d in range(docs - 1, -1, -1):
            end = jnp.where(position < ends_ref[d], ends_ref[d], end)
        return end

    dq_acc[...] = jnp.zeros_like(dq_acc)
    q_local = lax.broadcasted_iota(jnp.int32, (1, tile_q), 1)
    q_base = (q_local // piece) * run + core * piece + q_local % piece

    def key_step(kt, carry):
        k_lo = kt * tile_k
        rows = pl.ds(pl.multiple_of(k_lo, tile_k), tile_k)
        k = k_ref[rows, :]
        v = v_ref[rows, :]
        k_t = k.T
        k_pos = key_token(k_lo + lax.broadcasted_iota(jnp.int32, (tile_k, 1), 0))
        k_end = doc_end(k_pos)
        first = key_token(k_lo) // (2 * tile_q)
        last = (doc_end(key_token(k_lo + tile_k - 1)) - 1) // (2 * tile_q)
        dk_acc[...] = jnp.zeros_like(dk_acc)
        dv_acc[...] = jnp.zeros_like(dv_acc)

        def query_step(qt, carry):
            q_rows = pl.ds(pl.multiple_of(qt * tile_q, tile_q), tile_q)
            q = q_ref[q_rows, :]
            g = g_ref[q_rows, :]
            nd = nd_ref[qt]
            norm = nd[0:1, :]
            delta = nd[1:2, :]
            q_pos = q_base + qt * (2 * tile_q)
            s = dot(k, q, ((1,), (1,)))
            dp = dot(v, g, ((1,), (1,)))
            allowed = (k_pos <= q_pos) & (q_pos < k_end)
            p = jnp.where(allowed, jnp.exp2(s * (SCALING * LOG2E) - norm), 0.0)
            ds = (p * (dp - delta)).astype(jnp.bfloat16)
            dv_acc[...] += dot(p.astype(jnp.bfloat16), g, ((1,), (0,)))
            dk_acc[...] += dot(ds, q, ((1,), (0,)))
            dq_acc[qt] += dot(k_t, ds, ((1,), (0,)))
            return carry

        lax.fori_loop(first, last + 1, query_step, 0)
        dk_ref[rows, :] = (dk_acc[...] * SCALING).astype(jnp.bfloat16)
        dv_ref[rows, :] = dv_acc[...].astype(jnp.bfloat16)
        return carry

    lax.fori_loop(0, k_tiles, key_step, 0)

    def finish(qt, carry):
        q_rows = pl.ds(pl.multiple_of(qt * tile_q, tile_q), tile_q)
        dq_ref[q_rows, :] = (dq_acc[qt] * SCALING).T.astype(jnp.bfloat16)
        return carry

    lax.fori_loop(0, q_tiles, finish, 0)


def local_attention(piece, groups, ends, place, q, g, nd, k, v):
    tile_q = nd.shape[2]
    tile_k = min(TILE_K, k.shape[0])
    whole = pl.BlockSpec(memory_space=pltpu.VMEM)
    scalars = pl.BlockSpec(memory_space=pltpu.SMEM)
    return pl.pallas_call(
        functools.partial(attention_kernel, piece, groups, ends.shape[0]),
        out_shape=(
            jax.ShapeDtypeStruct(q.shape, jnp.bfloat16),
            jax.ShapeDtypeStruct(k.shape, jnp.bfloat16),
            jax.ShapeDtypeStruct(v.shape, jnp.bfloat16),
        ),
        in_specs=[scalars, scalars, whole, whole, whole, whole, whole],
        out_specs=(whole, whole, whole),
        scratch_shapes=[
            pltpu.VMEM((q.shape[0] // tile_q, HEAD_DIM, tile_q), jnp.float32),
            pltpu.VMEM((tile_k, HEAD_DIM), jnp.float32),
            pltpu.VMEM((tile_k, HEAD_DIM), jnp.float32),
        ],
        compiler_params=pltpu.CompilerParams(vmem_limit_bytes=58 * 1024 * 1024),
    )(ends, place, q, g, nd, k, v)


def per_device(sizes, query_states, key_states, value_states, saved_output, output_grad,
               normalizer, doc_lengths):
    yx, core, ko, head = (sizes[a] for a in Q_AXES)
    devices = yx * core * ko * head
    rows = query_states.shape[0]
    piece = rows // (yx * ko * core)
    groups = yx * ko
    row_delta = jnp.sum(
        (output_grad.astype(jnp.float32) * saved_output.astype(jnp.float32)).reshape(
            rows, KV_HEADS, HEAD_DIM
        ),
        axis=2,
    )

    def deal(x, key_side):
        x = x.reshape(yx, ko, core, piece, KV_HEADS, -1)
        order = (1, 4, 0, 2, 3, 5) if key_side else (0, 2, 1, 4, 3, 5)
        x = x.transpose(order).reshape(devices, piece, x.shape[-1])
        return lax.all_to_all(x, K_AXES if key_side else Q_AXES, 0, 0, tiled=True)

    def undeal(x, key_side):
        x = lax.all_to_all(x, K_AXES if key_side else Q_AXES, 0, 0, tiled=True)
        if key_side:
            x = x.reshape(ko, head, yx, core, piece, HEAD_DIM).transpose(2, 0, 3, 4, 1, 5)
        else:
            x = x.reshape(yx, core, ko, head, piece, HEAD_DIM).transpose(0, 2, 1, 4, 3, 5)
        return x.reshape(rows, KV_HEADS * HEAD_DIM)

    nd = jnp.stack([normalizer * LOG2E, row_delta], axis=-1)
    nd = deal(nd, False)
    q = deal(query_states, False)
    g = deal(output_grad, False)
    k = deal(key_states, True)
    v = deal(value_states, True)

    def gather(x, axes):
        x = lax.all_gather(x, axes, axis=0, tiled=False)
        return x.transpose(1, 0, 2, 3).reshape(-1, x.shape[-1])

    nd = gather(nd, ("yx", "ko"))
    q = gather(q, ("yx", "ko"))
    g = gather(g, ("yx", "ko"))
    k = gather(k, ("core",))
    v = gather(v, ("core",))
    tile_q = min(TILE_Q, q.shape[0])
    nd = nd.reshape(-1, tile_q, 2).transpose(0, 2, 1)
    place = jnp.stack(
        [lax.axis_index("core"), lax.axis_index("yx") * ko + lax.axis_index("ko")]
    ).astype(jnp.int32)
    ends = jnp.cumsum(doc_lengths)
    dq, dk, dv = local_attention(piece, groups, ends, place, q, g, nd, k, v)

    def total(x, parts, axes):
        x = x.reshape(devices, parts, piece, HEAD_DIM).transpose(1, 0, 2, 3)
        x = lax.all_to_all(x, axes, 0, 0, tiled=True)
        return jnp.sum(x.astype(jnp.float32), axis=0).astype(jnp.bfloat16)

    dq = undeal(total(dq, groups, ("yx", "ko")), False)
    dk = undeal(total(dk, core, ("core",)), True)
    dv = undeal(total(dv, core, ("core",)), True)
    return dq, dk, dv


def solution(mesh):
    qrow = mesh.shape["qrow"]
    kcol = mesh.shape["kcol"]
    sizes = {"yx": qrow // 2, "core": 2, "ko": kcol // KV_HEADS, "head": KV_HEADS}
    fine = Mesh(mesh.devices.reshape([sizes[a] for a in Q_AXES]), Q_AXES)
    by_query = P(Q_AXES, None)
    by_key = P(K_AXES, None)
    return jax.shard_map(
        functools.partial(per_device, sizes),
        mesh=fine,
        in_specs=(by_query, by_key, by_key, by_query, by_query, by_query, P()),
        out_specs=(by_query, by_key, by_key),
        check_vma=False,
    )
```

profile of v0, /device:TPU:26, one launch (start us, length us, event | category | flops | bytes accessed | tf_op | source)
XLA Modules:
  0.0 470.6 jit_solution(4373128552337968715)
XLA Ops:
  7.2 1.3 reshape.116
  8.8 29.8 %all_to_all.55 = bf16[32,128,128]{2,1,0:T(8,128)(2,1)} all-to-all(bf16[32,128,128]{2,1,0:T(8,128)(2,1)S(1)} %bitcast.89), channel_id=1, replica_groups=mesh['yx'=4,'core'=2,'ko'=1,'head'=4] {'ko','head','yx','core'}, dimensions={0} | all-to-all | bytes 2097152 | tf_op jit(solution)/shard_map/all_to_all | solution.py:138
  38.7 0.3 reshape.119
  39.3 29.7 %all_to_all.56 = bf16[32,128,128]{2,1,0:T(8,128)(2,1)} all-to-all(bf16[32,128,128]{2,1,0:T(8,128)(2,1)S(1)} %bitcast.90), channel_id=1, replica_groups=mesh['yx'=4,'core'=2,'ko'=1,'head'=4] {'ko','head','yx','core'}, dimensions={0} | all-to-all | bytes 2097152 | tf_op jit(solution)/shard_map/all_to_all | solution.py:138
  69.1 0.3 reshape.108
  69.4 0.2 copy.29
  69.6 30.3 %all_to_all.57 = bf16[32,128,128]{2,1,0:T(8,128)(2,1)} all-to-all(bf16[32,128,128]{2,1,0:T(8,128)(2,1)S(1)} %bitcast.91), channel_id=1, replica_groups=mesh['yx'=4,'core'=2,'ko'=1,'head'=4] {'yx','core','ko','head'}, dimensions={0} | all-to-all | bytes 2097152 | tf_op jit(solution)/shard_map/all_to_all | solution.py:138
  100.0 0.3 reshape.111
  100.6 29.5 %all_to_all.58 = bf16[32,128,128]{2,1,0:T(8,128)(2,1)} all-to-all(bf16[32,128,128]{2,1,0:T(8,128)(2,1)S(1)} %bitcast.92), channel_id=1, replica_groups=mesh['yx'=4,'core'=2,'ko'=1,'head'=4] {'yx','core','ko','head'}, dimensions={0} | all-to-all | bytes 2097152 | tf_op jit(solution)/shard_map/all_to_all | solution.py:138
  130.1 1.7 convert_multiply_fusion
  131.8 1.9 reshape.114
  133.7 1.1 reduce_sum.45
  135.1 0.6 copy.35
  135.8 4.9 %all-to-all-start.2 = ((f32[32,128,2]{1,2,0:T(2,128)}), f32[32,128,2]{1,2,0:T(2,128)S(1)}, u32[]{:S(2)}, u32[]{:S(2)}) async-start(f32[32,128,2]{1,2,0:T(2,128)} %copy.35), calls=%async_computation.2 | async-start | bytes 65536 | tf_op jit(solution)/shard_map/all_to_all | solution.py:138
  140.7 0.7 reduce-window.9
  141.4 0.6 pad_add_fusion.where_ref
  142.0 2.1 all-to-all-done.2
  144.1 9.7 %all-gather.2 = f32[128,128,2]{1,0,2:T(8,128)S(1)} all-gather(f32[32,128,2]{1,0,2:T(8,128)S(1)} %copy.36), channel_id=4, replica_groups=mesh['yx'=4,'core'=2,'ko'=1,'head'=4] {'yx','ko'}, dimensions={0}, use_global_device_ids=true | all-gather | bytes 163840 | tf_op jit(solution)/shard_map/all_gather | solution.py:156
  153.9 0.8 reshape_reshape.3
  154.7 3.2 copy.39
  157.9 3.1 copy.41
  161.0 1.1 all-gather.10.cloned.1.call-done
  162.1 4.7 %copy.30 = bf16[32,4,128,128]{3,2,1,0:T(8,128)(2,1)} copy(bf16[32,4,128,128]{3,2,0,1:T(8,128)(2,1)} %bitcast.83) | data formatting | bytes 8388608 | tf_op jit(solution)/shard_map/transpose | solution.py:157
  166.8 49.6 %all-gather.12.cloned.1.call-done = bf16[128,128,128]{2,1,0:T(8,128)(2,1)} async-done(((bf16[32,128,128]{2,1,0:T(8,128)(2,1)}), bf16[128,128,128]{2,1,0:T(8,128)(2,1)}) %all-gather.12.cloned.1.call-update) | async-done | bytes 4194320 | tf_op jit(solution)/shard_map/all_gather | solution.py:156
  216.4 4.8 %copy.32 = bf16[32,4,128,128]{3,2,1,0:T(8,128)(2,1)} copy(bf16[32,4,128,128]{3,2,0,1:T(8,128)(2,1)} %bitcast.84) | data formatting | bytes 8388608 | tf_op jit(solution)/shard_map/transpose | solution.py:157
  221.1 68.5 %shard_map.94 = (bf16[16384,128]{1,0:T(8,128)(2,1)}, bf16[8192,128]{1,0:T(8,128)(2,1)}, bf16[8192,128]{1,0:T(8,128)(2,1)}) custom-call(s32[8]{0:T(128)} %bitcast.110, s32[2]{0:T(128)} %pad_add_fusion.where_ref, bf16[16384,128]{1,0:T(8,128)(2,1)} %bitcast.76, bf16[16384,128]{1,0:T(8,128)(2,1)} %bitcast.77, f32[32,2,512]{2,1,0:T(2,128)} %bitcast.105, ...), custom_call_target="tpu_custom_call" | custom-call | tf_op jit(solution)/shard_map/pallas_call | solution.py:102
  289.6 3.2 copy.59
  292.8 3.8 all-to-all-start.7
  296.6 3.2 copy.58
  299.8 1.4 copy-done
  301.2 3.8 all-to-all-start.9
  304.9 3.3 reduce_sum.47
  308.3 17.7 %all-to-all-start.8 = ((bf16[32,128,128]{2,1,0:T(8,128)(2,1)}), bf16[32,128,128]{2,1,0:T(8,128)(2,1)S(1)}, u32[]{:S(2)}, u32[]{:S(2)}) async-start(bf16[32,128,128]{2,1,0:T(8,128)(2,1)} %reduce_sum.47), calls=%async_computation.8 | async-start | bytes 2097152 | tf_op jit(solution)/shard_map/all_to_all | solution.py:141
  326.0 4.8 %copy.57 = bf16[32,4,128,128]{3,2,0,1:T(8,128)(2,1)} copy(bf16[32,4,128,128]{3,2,1,0:T(8,128)(2,1)} %bitcast.85) | data formatting | bytes 8388608 | tf_op jit(solution)/shard_map/reshape | solution.py:173
  330.7 19.3 %all-to-all-done.8 = bf16[32,128,128]{2,1,0:T(8,128)(2,1)S(1)} async-done(((bf16[32,128,128]{2,1,0:T(8,128)(2,1)}), bf16[32,128,128]{2,1,0:T(8,128)(2,1)S(1)}, u32[]{:S(2)}, u32[]{:S(2)}) %all-to-all-start.8) | async-done | bytes 1048608 | tf_op jit(solution)/shard_map/all_to_all | solution.py:141
  350.0 5.2 %all-to-all-start.5 = ((bf16[4,32,128,128]{3,2,1,0:T(8,128)(2,1)}), bf16[4,32,128,128]{3,2,1,0:T(8,128)(2,1)}, u32[]{:S(2)}, u32[]{:S(2)}) async-start(bf16[4,32,128,128]{3,2,1,0:T(8,128)(2,1)} %bitcast.78), calls=%async_computation.5 | async-start | bytes 8388608 | tf_op jit(solution)/shard_map/all_to_all | solution.py:174
  355.2 1.7 reduce_sum.48
  356.9 45.5 %all-to-all-done.5 = bf16[4,32,128,128]{3,2,1,0:T(8,128)(2,1)} async-done(((bf16[4,32,128,128]{3,2,1,0:T(8,128)(2,1)}), bf16[4,32,128,128]{3,2,1,0:T(8,128)(2,1)}, u32[]{:S(2)}, u32[]{:S(2)}) %all-to-all-start.5) | async-done | bytes 4194336 | tf_op jit(solution)/shard_map/all_to_all | solution.py:174
  402.5 5.2 %all-to-all-start.10 = ((bf16[32,128,128]{2,1,0:T(8,128)(2,1)}), bf16[32,128,128]{2,1,0:T(8,128)(2,1)S(1)}, u32[]{:S(2)}, u32[]{:S(2)}) async-start(bf16[32,128,128]{2,1,0:T(8,128)(2,1)} %reduce_sum.48), calls=%async_computation.10 | async-start | bytes 2097152 | tf_op jit(solution)/shard_map/all_to_all | solution.py:141
  407.7 4.3 reduce_sum.46
  411.9 19.8 %all-to-all-done.10 = bf16[32,128,128]{2,1,0:T(8,128)(2,1)S(1)} async-done(((bf16[32,128,128]{2,1,0:T(8,128)(2,1)}), bf16[32,128,128]{2,1,0:T(8,128)(2,1)S(1)}, u32[]{:S(2)}, u32[]{:S(2)}) %all-to-all-start.10) | async-done | bytes 1048608 | tf_op jit(solution)/shard_map/all_to_all | solution.py:141
  431.7 5.8 %all-to-all-start.6 = ((bf16[32,128,128]{2,1,0:T(8,128)(2,1)}), bf16[32,128,128]{2,1,0:T(8,128)(2,1)S(1)}, u32[]{:S(2)}, u32[]{:S(2)}) async-start(bf16[32,128,128]{2,1,0:T(8,128)(2,1)} %reduce_sum.46), calls=%async_computation.6 | async-start | bytes 2097152 | tf_op jit(solution)/shard_map/all_to_all | solution.py:141
  437.5 0.8 copy.45
  438.3 0.8 copy.47
  439.2 1.7 copy_bitcast_fusion.3
  440.9 21.2 %all-to-all-done.6 = bf16[32,128,128]{2,1,0:T(8,128)(2,1)S(1)} async-done(((bf16[32,128,128]{2,1,0:T(8,128)(2,1)}), bf16[32,128,128]{2,1,0:T(8,128)(2,1)S(1)}, u32[]{:S(2)}, u32[]{:S(2)}) %all-to-all-start.6) | async-done | bytes 1048608 | tf_op jit(solution)/shard_map/all_to_all | solution.py:141
  462.1 0.8 copy.43
  462.9 1.2 copy.60
  (34 shorter events, 1.3 us)
Async XLA Ops:
  7.2 147.5 %all-gather.14.cloned.1.call-start = ((), (), s32[]{:S(2)}) async-start(), calls=%async_computation.13 | async-start | bytes 3145728 | tf_op jit(solution)/shard_map/all_gather | solution.py:156
  8.8 29.9 %copy-start.2 = (bf16[1024,512]{1,0:T(8,128)(2,1)S(1)}, bf16[1024,512]{1,0:T(8,128)(2,1)}, u32[]{:S(2)}) copy-start(bf16[1024,512]{1,0:T(8,128)(2,1)} %param.9) | copy-start | bytes 3145732
  38.6 119.2 %all-gather.16.cloned.1.call-start = ((), (), s32[]{:S(2)}) async-start(), calls=%async_computation.14 | async-start | bytes 3145728 | tf_op jit(solution)/shard_map/all_gather | solution.py:156
  39.2 29.8 %copy-start.3 = (bf16[1024,512]{1,0:T(8,128)(2,1)S(1)}, bf16[1024,512]{1,0:T(8,128)(2,1)}, u32[]{:S(2)}) copy-start(bf16[1024,512]{1,0:T(8,128)(2,1)} %param.7) | copy-start | bytes 3145732
  69.0 93.1 %all-gather.10.cloned.1.call-start = ((), (), s32[]{:S(2)}) async-start(), calls=%async_computation.11 | async-start | bytes 5242880 | tf_op jit(solution)/shard_map/all_gather | solution.py:156
  69.6 30.4 %copy-start.1 = (bf16[1024,512]{1,0:T(8,128)(2,1)S(1)}, bf16[1024,512]{1,0:T(8,128)(2,1)}, u32[]{:S(2)}) copy-start(bf16[1024,512]{1,0:T(8,128)(2,1)} %param.11) | copy-start | bytes 3145732
  99.9 116.4 %all-gather.12.cloned.1.call-start = ((), (), s32[]{:S(2)}) async-start(), calls=%async_computation.12 | async-start | bytes 5242880 | tf_op jit(solution)/shard_map/all_gather | solution.py:156
  100.6 29.5 %copy-start.4 = (bf16[1024,512]{1,0:T(8,128)(2,1)S(1)}, bf16[1024,512]{1,0:T(8,128)(2,1)}, u32[]{:S(2)}) copy-start(bf16[1024,512]{1,0:T(8,128)(2,1)} %param.10) | copy-start | bytes 3145732
  133.7 1.4 copy-start.5
  133.7 7.0 %copy-start.6 = (s32[8]{0:T(128)S(1)}, s32[8]{0:T(128)}, u32[]{:S(2)}) copy-start(s32[8]{0:T(128)} %param.13) | copy-start | bytes 100
  135.8 8.4 %all-to-all-start.2 = ((f32[32,128,2]{1,2,0:T(2,128)}), f32[32,128,2]{1,2,0:T(2,128)S(1)}, u32[]{:S(2)}, u32[]{:S(2)}) async-start(f32[32,128,2]{1,2,0:T(2,128)} %copy.35), calls=%async_computation.2 | async-start | bytes 65536 | tf_op jit(solution)/shard_map/all_to_all | solution.py:138
  292.8 7.0 %all-to-all-start.7 = ((bf16[2,32,128,128]{3,2,1,0:T(8,128)(2,1)}), bf16[2,32,128,128]{3,2,1,0:T(8,128)(2,1)S(1)}, u32[]{:S(2)}, u32[]{:S(2)}) async-start(bf16[2,32,128,128]{3,2,1,0:T(8,128)(2,1)} %bitcast.82), calls=%async_computation.7 | async-start | bytes 4194304 | tf_op jit(solution)/shard_map/all_to_all | solution.py:174
  299.8 1.4 copy-start
  301.2 7.1 %all-to-all-start.9 = ((bf16[2,32,128,128]{3,2,1,0:T(8,128)(2,1)}), bf16[2,32,128,128]{3,2,1,0:T(8,128)(2,1)S(1)}, u32[]{:S(2)}, u32[]{:S(2)}) async-start(bf16[2,32,128,128]{3,2,1,0:T(8,128)(2,1)} %bitcast.81), calls=%async_computation.9 | async-start | bytes 4194304 | tf_op jit(solution)/shard_map/all_to_all | solution.py:174
  308.3 41.7 %all-to-all-start.8 = ((bf16[32,128,128]{2,1,0:T(8,128)(2,1)}), bf16[32,128,128]{2,1,0:T(8,128)(2,1)S(1)}, u32[]{:S(2)}, u32[]{:S(2)}) async-start(bf16[32,128,128]{2,1,0:T(8,128)(2,1)} %reduce_sum.47), calls=%async_computation.8 | async-start | bytes 2097152 | tf_op jit(solution)/shard_map/all_to_all | solution.py:141
  350.0 52.5 %all-to-all-start.5 = ((bf16[4,32,128,128]{3,2,1,0:T(8,128)(2,1)}), bf16[4,32,128,128]{3,2,1,0:T(8,128)(2,1)}, u32[]{:S(2)}, u32[]{:S(2)}) async-start(bf16[4,32,128,128]{3,2,1,0:T(8,128)(2,1)} %bitcast.78), calls=%async_computation.5 | async-start | bytes 8388608 | tf_op jit(solution)/shard_map/all_to_all | solution.py:174
  402.5 29.2 %all-to-all-start.10 = ((bf16[32,128,128]{2,1,0:T(8,128)(2,1)}), bf16[32,128,128]{2,1,0:T(8,128)(2,1)S(1)}, u32[]{:S(2)}, u32[]{:S(2)}) async-start(bf16[32,128,128]{2,1,0:T(8,128)(2,1)} %reduce_sum.48), calls=%async_computation.10 | async-start | bytes 2097152 | tf_op jit(solution)/shard_map/all_to_all | solution.py:141
  431.7 30.4 %all-to-all-start.6 = ((bf16[32,128,128]{2,1,0:T(8,128)(2,1)}), bf16[32,128,128]{2,1,0:T(8,128)(2,1)S(1)}, u32[]{:S(2)}, u32[]{:S(2)}) async-start(bf16[32,128,128]{2,1,0:T(8,128)(2,1)} %reduce_sum.46), calls=%async_computation.6 | async-start | bytes 2097152 | tf_op jit(solution)/shard_map/all_to_all | solution.py:141
Sparse Core Ops, SparseCore 0:
  38.8 11.7 all-gather.13
  69.1 11.7 all-gather.15
  100.1 61.9 all-gather.9
  163.8 52.5 all-gather.11
where the time goes:
time: 477 us; the launch traced here: 471 us
  waiting for transfers between devices  159 us (33%)
  blocking collectives  129 us (27%)
  Pallas kernels  68.5 us (14%)
  starting transfers between devices  46.5 us (10%)
  local copies, waits for them, and re-layouts  40.5 us (8%)
  between operations  14 us (3%)
  other arithmetic  13.4 us (3%)
    all_to_all x4, blocking collectives, deal(): return lax.all_to_all(x, K_AXES if key_side else Q_AXES, 0, 0, tiled=True)  119 us
    pallas_call x1, Pallas kernels, local_attention(): pl.pallas_call(functools.partial(attention_kernel, piece, groups, ends.sh...  68.5 us
    all_to_all x3, waiting for transfers between devices, undeal(): x = lax.all_to_all(x, K_AXES if key_side else Q_AXES, 0, 0, tiled=True)  60.2 us
    all_gather x4, waiting for transfers between devices, gather(): x = lax.all_gather(x, axes, axis=0, tiled=False)  50.6 us
    all_to_all x3, waiting for transfers between devices, total(): x = lax.all_to_all(x, axes, 0, 0, tiled=True)  45.5 us
    all_to_all x3, starting transfers between devices, undeal(): x = lax.all_to_all(x, K_AXES if key_side else Q_AXES, 0, 0, tiled=True)  28.7 us
    transpose x5, local copies, waits for them, and re-layouts, gather(): return x.transpose(1, 0, 2, 3).reshape(-1, x.shape[-1])  15.9 us
    all_to_all x3, starting transfers between devices, total(): x = lax.all_to_all(x, axes, 0, 0, tiled=True)  12.8 us
  transfers between devices with their start and end apart: 11, of which 7 were waited for; matrix products, arithmetic and copies ran while one was open for 9% of the time, Pallas kernels for 0%

commit v1 on v0

--- a/solution.py
+++ b/solution.py
@@ -10,20 +10,421 @@
 
 HEAD_DIM = 128
 KV_HEADS = 4
-TILE_Q = 512
-TILE_K = 256
+MOST = 8192
 SCALING = HEAD_DIM ** (-0.5)
 LOG2E = math.log2(math.e)
-
+MESH = pl.DeviceIdType.MESH
+TILE_K = 512
+
+
+def dot(a, b, dims):
+    return lax.dot_general(a, b, (dims, ((), ())), preferred_element_type=jnp.float32)
+
+
+def spread_kernel(
+    planes, q_ref, g_ref, nd_ref, k_ref, v_ref, qo, go, ndo, ko, vo,
+    send, recv, relay, kv_send, kv_recv, fwd_send, fwd_recv,
+):
+    row = lax.axis_index("qrow")
+    z = lax.axis_index("kcol")
+    s = row // 2
+    core = row % 2
+    tile = q_ref.shape[0] // 2
+    heads = KV_HEADS
+    partner = s * 2 + 1 - core
+    below = jnp.minimum(jnp.maximum(s - z, 0), 1)
+    plane = s - below
+    slot = core * planes + z
+
+    def query_parts(h, half):
+        rows = pl.ds(half * tile, tile)
+        cols = pl.ds(pl.multiple_of(h * HEAD_DIM, HEAD_DIM), HEAD_DIM)
+        return q_ref.at[rows, cols], g_ref.at[rows, cols], nd_ref.at[h, half]
+
+    def query_dst(which, j):
+        return qo.at[which, j], go.at[which, j], ndo.at[which, j]
+
+    def query_send(i, half, act):
+        h = (s + i) % heads
+        to = h * 2 + (z + half) % 2
+        home = (to == row) & (plane == z)
+        for t, (a, b) in enumerate(zip(query_parts(h, half), query_dst(below, slot))):
+            there = pltpu.make_async_remote_copy(
+                a, b, send.at[t, i, half], recv.at[t, below, slot],
+                device_id=(to, plane), device_id_type=MESH)
+            if act == "start":
+                pl.when(home)(pltpu.make_async_copy(a, b, recv.at[t, below, slot]).start)
+                pl.when(jnp.logical_not(home))(there.start)
+            else:
+                pl.when(jnp.logical_not(home))(there.wait_send)
+
+    def key_send(i, act):
+        h = (s + i) % heads
+        cols = pl.ds(pl.multiple_of(h * HEAD_DIM, HEAD_DIM), HEAD_DIM)
+        for t, (a, b) in enumerate(((k_ref, ko), (v_ref, vo))):
+            if i == 0:
+                if act == "start":
+                    pltpu.make_async_copy(a.at[:, cols], b.at[row], kv_recv.at[t, s]).start()
+            else:
+                there = pltpu.make_async_remote_copy(
+                    a.at[:, cols], b.at[row], kv_send.at[t, i], kv_recv.at[t, s],
+                    device_id=(h * 2 + core, z), device_id_type=MESH)
+                there.start() if act == "start" else there.wait_send()
+
+    def arrived(which, j):
+        for t, b in enumerate(query_dst(which, j)):
+            pltpu.make_async_copy(b, b, recv.at[t, which, j]).wait()
+
+    def pass_on(which, j, act):
+        to = z - 1 + 2 * which
+        for t, (a, b) in enumerate(zip(query_dst(which, j), query_dst(1 - which, j))):
+            copy = pltpu.make_async_remote_copy(
+                a, b, relay.at[t, which, j], recv.at[t, 1 - which, j],
+                device_id=(row, to), device_id_type=MESH)
+            copy.start() if act == "start" else copy.wait_send()
+
+    def key_forward(i, act):
+        src = (s + i) % heads
+        for t, b in enumerate((ko, vo)):
+            at = b.at[src * 2 + core]
+            copy = pltpu.make_async_remote_copy(
+                at, at, fwd_send.at[t, i], fwd_recv.at[t, src],
+                device_id=(partner, z), device_id_type=MESH)
+            if act == "start":
+                pltpu.make_async_copy(at, at, kv_recv.at[t, src]).wait()
+                copy.start()
+            else:
+                copy.wait_send()
+                got = b.at[src * 2 + 1 - core]
+                pltpu.make_async_copy(got, got, fwd_recv.at[t, src]).wait()
+
+    for i in range(heads):
+        for half in range(2):
+            query_send(i, half, "start")
+        key_send(i, "start")
+
+    def direct(j, z0, act):
+        @pl.when((z0 >= z))
+        def _():
+            if act == "start":
+                arrived(0, j)
+
+            @pl.when(z >= 1)
+            def _():
+                pass_on(0, j, act)
+
+        @pl.when((z0 <= z) & (z + 1 < planes))
+        def _():
+            if act == "start":
+                arrived(1, j)
+            pass_on(1, j, act)
+
+    for z0 in range(planes):
+        for c0 in range(2):
+            direct(c0 * planes + z0, z0, "start")
+    for i in range(heads):
+        key_forward(i, "start")
+    for z0 in range(planes):
+        for c0 in range(2):
+            j = c0 * planes + z0
+            pl.when(z0 < z)(functools.partial(arrived, 0, j))
+            pl.when((z0 > z) & (z + 1 < planes))(functools.partial(arrived, 1, j))
+    for i in range(heads):
+        for half in range(2):
+            query_send(i, half, "wait")
+        key_send(i, "wait")
+        key_forward(i, "wait")
+    for z0 in range(planes):
+        for c0 in range(2):
+            direct(c0 * planes + z0, z0, "wait")
+
+
+def spread(planes, q, g, nd, k, v):
+    n = q.shape[0]
+    slots = 2 * planes
+    anywhere = pl.BlockSpec(memory_space=pl.ANY)
+    whole = pl.BlockSpec(memory_space=pltpu.VMEM)
+    dma = pltpu.SemaphoreType.DMA
+    tiles = jax.ShapeDtypeStruct((2, slots, n // 2, HEAD_DIM), jnp.bfloat16)
+    keys = jax.ShapeDtypeStruct((2 * KV_HEADS, n, HEAD_DIM), jnp.bfloat16)
+    return pl.pallas_call(
+        functools.partial(spread_kernel, planes),
+        out_shape=(tiles, tiles, jax.ShapeDtypeStruct((2, slots, 2, n // 2), jnp.float32), keys, keys),
+        in_specs=[anywhere] * 5,
+        out_specs=(whole,) * 5,
+        scratch_shapes=[
+            dma((3, KV_HEADS, 2)), dma((3, 2, slots)), dma((3, 2, slots)),
+            dma((2, KV_HEADS)), dma((2, KV_HEADS)), dma((2, KV_HEADS)), dma((2, KV_HEADS)),
+        ],
+        compiler_params=pltpu.CompilerParams(
+            has_side_effects=True, vmem_limit_bytes=40 * 1024 * 1024),
+        name="spread",
+    )(q, g, nd, k, v)
+
+
+def attention_kernel(
+    docs, ends_ref, q_ref, g_ref, nd_ref, k_ref, v_ref, dq_ref, dk_ref, dv_ref,
+    dq_acc, dk_acc, dv_acc,
+):
+    slots, tile_q = q_ref.shape[1], q_ref.shape[2]
+    segment = dk_acc.shape[0]
+    tile_k = dk_tile = min(TILE_K, segment)
+    core = lax.axis_index("qrow") % 2
+    base = lax.axis_index("kcol") * segment
+
+    def doc_start(position):
+        start = jnp.zeros_like(position)
+        for d in range(docs):
+            start = jnp.where(position >= ends_ref[d], ends_ref[d], start)
+        return start
+
+    dk_acc[...] = jnp.zeros_like(dk_acc)
+    dv_acc[...] = jnp.zeros_like(dv_acc)
+
+    def query_step(i, carry):
+        which = i // slots
+        j = i % slots
+        q_lo = which * segment + (2 * j + (core + j) % 2) * tile_q
+        q_pos = q_lo + lax.broadcasted_iota(jnp.int32, (1, tile_q), 1)
+        q_start = doc_start(q_pos + base) - base
+        lo = jnp.maximum(doc_start(q_lo + base) - base, 0)
+        hi = jnp.minimum(q_lo + tile_q, segment)
+        last_start = jnp.maximum(doc_start(q_lo + base + tile_q - 1) - base, 0)
+        first = lo // tile_k
+        last = (hi + tile_k - 1) // tile_k
+        full_lo = jnp.minimum((last_start + tile_k - 1) // tile_k, last)
+        full_hi = jnp.maximum(jnp.minimum((q_lo + 1) // tile_k, last), full_lo)
+        q = q_ref[which, j]
+        g = g_ref[which, j]
+        nd = nd_ref[which, j]
+        norm = nd[0:1, :]
+        delta = nd[1:2, :]
+        dq_acc[...] = jnp.zeros_like(dq_acc)
+
+        def key_step(masked, kt, carry):
+            rows = pl.ds(pl.multiple_of(kt * tile_k, tile_k), tile_k)
+            k = k_ref[rows, :]
+            v = v_ref[rows, :]
+            s = dot(k, q, ((1,), (1,)))
+            dp = dot(v, g, ((1,), (1,)))
+            p = jnp.exp2(s * (SCALING * LOG2E) - norm)
+            if masked:
+                k_pos = kt * tile_k + lax.broadcasted_iota(jnp.int32, (tile_k, 1), 0)
+                p = jnp.where((k_pos <= q_pos) & (k_pos >= q_start), p, 0.0)
+            ds = (p * (dp - delta)).astype(jnp.bfloat16)
+            dv_acc[rows, :] += dot(p.astype(jnp.bfloat16), g, ((1,), (0,)))
+            dk_acc[rows, :] += dot(ds, q, ((1,), (0,)))
+            dq_acc[...] += dot(k, ds, ((0,), (0,)))
+            return carry
+
+        @pl.when(lo < hi)
+        def _():
+            lax.fori_loop(first, full_lo, functools.partial(key_step, True), 0)
+            lax.fori_loop(full_lo, full_hi, functools.partial(key_step, False), 0)
+            lax.fori_loop(full_hi, last, functools.partial(key_step, True), 0)
+
+        dq_ref[which, j] = (dq_acc[...] * SCALING).T.astype(jnp.bfloat16)
+        return carry
+
+    lax.fori_loop(0, 2 * slots, query_step, 0)
+
+    def finish(kt, carry):
+        rows = pl.ds(pl.multiple_of(kt * tile_k, tile_k), tile_k)
+        dk_ref[rows, :] = (dk_acc[rows, :] * SCALING).astype(jnp.bfloat16)
+        dv_ref[rows, :] = dv_acc[rows, :].astype(jnp.bfloat16)
+        return carry
+
+    lax.fori_loop(0, segment // tile_k, finish, 0)
+
+
+def attention(ends, q, g, nd, k, v):
+    tile_q = q.shape[2]
+    segment = k.shape[0]
+    whole = pl.BlockSpec(memory_space=pltpu.VMEM)
+    scalars = pl.BlockSpec(memory_space=pltpu.SMEM)
+    return pl.pallas_call(
+        functools.partial(attention_kernel, ends.shape[0]),
+        out_shape=(
+            jax.ShapeDtypeStruct(q.shape, jnp.bfloat16),
+            jax.ShapeDtypeStruct(k.shape, jnp.bfloat16),
+            jax.ShapeDtypeStruct(v.shape, jnp.bfloat16),
+        ),
+        in_specs=[scalars] + [whole] * 5,
+        out_specs=(whole,) * 3,
+        scratch_shapes=[
+            pltpu.VMEM((HEAD_DIM, tile_q), jnp.float32),
+            pltpu.VMEM((segment, HEAD_DIM), jnp.float32),
+            pltpu.VMEM((segment, HEAD_DIM), jnp.float32),
+        ],
+        compiler_params=pltpu.CompilerParams(vmem_limit_bytes=58 * 1024 * 1024),
+        name="attention",
+    )(ends, q, g, nd, k, v)
+
+
+def collect_kernel(
+    planes, dq_ref, dk_ref, dv_ref, dqo, dko, dvo, parts, pair, summed,
+    send, recv, pair_send, pair_recv, kv_send, kv_recv,
+):
+    row = lax.axis_index("qrow")
+    z = lax.axis_index("kcol")
+    s = row // 2
+    core = row % 2
+    heads = KV_HEADS
+    tile = dq_ref.shape[2]
+    n = dko.shape[0]
+    partner = s * 2 + 1 - core
+    mine = pl.ds(pl.multiple_of(s * HEAD_DIM, HEAD_DIM), HEAD_DIM)
+    kv = ((dk_ref, dko), (dv_ref, dvo))
+
+    def trade(i, act):
+        to = (s + 1 + i) % heads
+        for t, (a, _) in enumerate(kv):
+            copy = pltpu.make_async_remote_copy(
+                a.at[to * 2 + 1 - core], pair.at[t, to], pair_send.at[t, to], pair_recv.at[t, to],
+                device_id=(partner, z), device_id_type=MESH)
+            copy.start() if act == "start" else copy.wait_send()
+
+    def query_return(which, c0, z0, act):
+        j = c0 * planes + z0
+        half = (core + z0) % 2
+        to = (z + which) * 2 + c0
+        home = (to == row) & (z0 == z)
+        copy = pltpu.make_async_remote_copy(
+            dq_ref.at[which, j], parts.at[which, s, half],
+            send.at[which, j], recv.at[which, s, half],
+            device_id=(to, z0), device_id_type=MESH)
+
+        def move():
+            if act == "start":
+                @pl.when(home)
+                def _():
+                    parts[which, s, half] = dq_ref[which, j]
+                pl.when(jnp.logical_not(home))(copy.start)
+            else:
+                pl.when(jnp.logical_not(home))(copy.wait_send)
+        if which == 0:
+            move()
+        else:
+            pl.when(z + 1 < planes)(move)
+
+    def every_query(act):
+        for dz in range(planes):
+            for c0 in range(2):
+                for which in range(2):
+                    query_return(which, c0, dz, act)
+
+    for i in range(heads):
+        trade(i, "start")
+    every_query("start")
+
+    def key_return(i, act):
+        to = (s + 1 + i) % heads
+        if i == heads - 1 and act != "sum":
+            return
+        for t, (a, out) in enumerate(kv):
+            if act == "sum":
+                got = pair.at[t, to]
+                pltpu.make_async_copy(got, got, pair_recv.at[t, to]).wait()
+                total = (a[to * 2 + core].astype(jnp.float32)
+                         + pair[t, to].astype(jnp.float32)).astype(jnp.bfloat16)
+                if i == heads - 1:
+                    out[:, mine] = total
+                else:
+                    summed[t, to] = total
+            else:
+                copy = pltpu.make_async_remote_copy(
+                    summed.at[t, to], out.at[:, mine], kv_send.at[t, to], kv_recv.at[t, s],
+                    device_id=(to * 2 + core, z), device_id_type=MESH)
+                copy.start() if act == "start" else copy.wait_send()
+
+    for i in range(heads):
+        key_return(i, "sum")
+        if i:
+            key_return(i - 1, "start")
+
+    def add_up(h, half):
+        home = (h == s) & (z == s) & (half == (core + z) % 2)
+        home_next = (h == s) & (s == z + 1) & (half == (core + z) % 2)
+        got = parts.at[0, h, half]
+        pl.when(jnp.logical_not(home))(pltpu.make_async_copy(got, got, recv.at[0, h, half]).wait)
+        rows = pl.ds(half * tile, tile)
+        cols = pl.ds(h * HEAD_DIM, HEAD_DIM)
+
+        @pl.when(s == 0)
+        def _():
+            dqo[rows, cols] = parts[0, h, half]
+
+        @pl.when(s > 0)
+        def _():
+            more = parts.at[1, h, half]
+            pl.when(jnp.logical_not(home_next))(
+                pltpu.make_async_copy(more, more, recv.at[1, h, half]).wait)
+            dqo[rows, cols] = (parts[0, h, half].astype(jnp.float32)
+                               + parts[1, h, half].astype(jnp.float32)).astype(jnp.bfloat16)
+
+    for h in range(heads):
+        for half in range(2):
+            add_up(h, half)
+    for i in range(heads):
+        trade(i, "wait")
+        key_return(i, "wait")
+    every_query("wait")
+    for i in range(heads - 1):
+        src = (s + 1 + i) % heads
+        cols = pl.ds(pl.multiple_of(src * HEAD_DIM, HEAD_DIM), HEAD_DIM)
+        for t, (_, out) in enumerate(kv):
+            got = out.at[:, cols]
+            pltpu.make_async_copy(got, got, kv_recv.at[t, src]).wait()
+
+
+def collect(planes, dq, dk, dv):
+    tile = dq.shape[2]
+    n = dk.shape[1]
+    whole = pl.BlockSpec(memory_space=pltpu.VMEM)
+    dma = pltpu.SemaphoreType.DMA
+    out = jax.ShapeDtypeStruct((n, KV_HEADS * HEAD_DIM), jnp.bfloat16)
+    return pl.pallas_call(
+        functools.partial(collect_kernel, planes),
+        out_shape=(out,) * 3,
+        in_specs=[whole] * 3,
+        out_specs=(whole,) * 3,
+        scratch_shapes=[
+            pltpu.VMEM((2, KV_HEADS, 2, tile, HEAD_DIM), jnp.bfloat16),
+            pltpu.VMEM((2, KV_HEADS, n, HEAD_DIM), jnp.bfloat16),
+            pltpu.VMEM((2, KV_HEADS, n, HEAD_DIM), jnp.bfloat16),
+            dma((2, 2 * planes)), dma((2, KV_HEADS, 2)),
+            dma((2, KV_HEADS)), dma((2, KV_HEADS)), dma((2, KV_HEADS)), dma((2, KV_HEADS)),
+        ],
+        compiler_params=pltpu.CompilerParams(
+            has_side_effects=True, vmem_limit_bytes=40 * 1024 * 1024),
+        name="collect",
+    )(dq, dk, dv)
+
+
+def by_segment(planes, query_states, key_states, value_states, saved_output, output_grad,
+               normalizer, doc_lengths):
+    n = query_states.shape[0]
+    row_delta = jnp.sum(
+        (output_grad.astype(jnp.float32) * saved_output.astype(jnp.float32)).reshape(
+            n, KV_HEADS, HEAD_DIM
+        ),
+        axis=2,
+    )
+    nd = jnp.stack([normalizer * LOG2E, row_delta], axis=0)
+    nd = nd.reshape(2, 2, n // 2, KV_HEADS).transpose(3, 1, 0, 2)
+    q, g, nd, k, v = spread(planes, query_states, output_grad, nd, key_states, value_states)
+    ends = jnp.cumsum(doc_lengths)
+    dq, dk, dv = attention(ends, q, g, nd, k.reshape(-1, HEAD_DIM), v.reshape(-1, HEAD_DIM))
+    return collect(planes, dq, dk.reshape(-1, n, HEAD_DIM), dv.reshape(-1, n, HEAD_DIM))
+
+
+DEAL_Q = 512
+DEAL_K = 256
 Q_AXES = ("yx", "core", "ko", "head")
 K_AXES = ("ko", "head", "yx", "core")
 
 
-def dot(a, b, dims):
-    return lax.dot_general(a, b, (dims, ((), ())), preferred_element_type=jnp.float32)
-
-
-def attention_kernel(
+def dealt_kernel(
     piece, groups, docs, ends_ref, where_ref, q_ref, g_ref, nd_ref, k_ref, v_ref,
     dq_ref, dk_ref, dv_ref, dq_acc, dk_acc, dv_acc,
 ):
@@ -94,13 +495,13 @@
     lax.fori_loop(0, q_tiles, finish, 0)
 
 
-def local_attention(piece, groups, ends, place, q, g, nd, k, v):
+def dealt_attention(piece, groups, ends, place, q, g, nd, k, v):
     tile_q = nd.shape[2]
-    tile_k = min(TILE_K, k.shape[0])
+    tile_k = min(DEAL_K, k.shape[0])
     whole = pl.BlockSpec(memory_space=pltpu.VMEM)
     scalars = pl.BlockSpec(memory_space=pltpu.SMEM)
     return pl.pallas_call(
-        functools.partial(attention_kernel, piece, groups, ends.shape[0]),
+        functools.partial(dealt_kernel, piece, groups, ends.shape[0]),
         out_shape=(
             jax.ShapeDtypeStruct(q.shape, jnp.bfloat16),
             jax.ShapeDtypeStruct(k.shape, jnp.bfloat16),
@@ -161,13 +562,13 @@
     g = gather(g, ("yx", "ko"))
     k = gather(k, ("core",))
     v = gather(v, ("core",))
-    tile_q = min(TILE_Q, q.shape[0])
+    tile_q = min(DEAL_Q, q.shape[0])
     nd = nd.reshape(-1, tile_q, 2).transpose(0, 2, 1)
     place = jnp.stack(
         [lax.axis_index("core"), lax.axis_index("yx") * ko + lax.axis_index("ko")]
     ).astype(jnp.int32)
     ends = jnp.cumsum(doc_lengths)
-    dq, dk, dv = local_attention(piece, groups, ends, place, q, g, nd, k, v)
+    dq, dk, dv = dealt_attention(piece, groups, ends, place, q, g, nd, k, v)
 
     def total(x, parts, axes):
         x = x.reshape(devices, parts, piece, HEAD_DIM).transpose(1, 0, 2, 3)
@@ -183,14 +584,23 @@
 def solution(mesh):
     qrow = mesh.shape["qrow"]
     kcol = mesh.shape["kcol"]
-    sizes = {"yx": qrow // 2, "core": 2, "ko": kcol // KV_HEADS, "head": KV_HEADS}
-    fine = Mesh(mesh.devices.reshape([sizes[a] for a in Q_AXES]), Q_AXES)
-    by_query = P(Q_AXES, None)
-    by_key = P(K_AXES, None)
-    return jax.shard_map(
-        functools.partial(per_device, sizes),
-        mesh=fine,
-        in_specs=(by_query, by_key, by_key, by_query, by_query, by_query, P()),
-        out_specs=(by_query, by_key, by_key),
-        check_vma=False,
-    )
+
+    def whole(*args):
+        tokens = args[0].shape[0]
+        if qrow == 2 * KV_HEADS and kcol == KV_HEADS and tokens // kcol >= MOST:
+            by_query, by_key = P(("qrow", "kcol"), None), P(("kcol", "qrow"), None)
+            place, body = mesh, functools.partial(by_segment, kcol)
+        else:
+            sizes = {"yx": qrow // 2, "core": 2, "ko": kcol // KV_HEADS, "head": KV_HEADS}
+            place = Mesh(mesh.devices.reshape([sizes[a] for a in Q_AXES]), Q_AXES)
+            by_query, by_key = P(Q_AXES, None), P(K_AXES, None)
+            body = functools.partial(per_device, sizes)
+        return jax.shard_map(
+            body,
+            mesh=place,
+            in_specs=(by_query, by_key, by_key, by_query, by_query, by_query, P()),
+            out_specs=(by_query, by_key, by_key),
+            check_vma=False,
+        )(*args)
+
+    return whole

time: 477 us -> 329 us (0.69)
  Pallas kernels: 68.5 us -> 300 us
  waiting for transfers between devices: 159 us -> 0 us
  blocking collectives: 129 us -> 0 us
  starting transfers between devices: 46.5 us -> 0 us
  local copies, waits for them, and re-layouts: 40.5 us -> 17.9 us
  between operations: 14 us -> 0.72 us
  other arithmetic: 13.4 us -> 7.67 us
    pallas_call x1 -> x3, Pallas kernels: 68.5 us -> 300 us  [the longest x1 154 us: collect(): pl.pallas_call(functools.partial(collect_kernel, planes), out_shape=(out,...]
    all_to_all x4 -> x0, blocking collectives: 119 us -> none  [deal(): return lax.all_to_all(x, K_AXES if key_side else Q_AXES, 0, 0, tiled=True)]
    all_to_all x7 -> x0, waiting for transfers between devices: 108 us -> none  [the longest x3 60.2 us: undeal(): x = lax.all_to_all(x, K_AXES if key_side else Q_AXES, 0, 0, tiled=True)]
    all_gather x4 -> x0, waiting for transfers between devices: 50.6 us -> none  [gather(): x = lax.all_gather(x, axes, axis=0, tiled=False)]
    all_to_all x7 -> x0, starting transfers between devices: 46.4 us -> none  [the longest x3 28.7 us: undeal(): x = lax.all_to_all(x, K_AXES if key_side else Q_AXES, 0, 0, tiled=True)]
    transpose x13 -> x0, local copies, waits for them, and re-layouts: 19.3 us -> none  [the longest x5 15.9 us: gather(): return x.transpose(1, 0, 2, 3).reshape(-1, x.shape[-1])]
    reshape x10 -> x1, local copies, waits for them, and re-layouts: 17.7 us -> 1.77 us  [by_segment(): (output_grad.astype(jnp.float32) * saved_output.astype(jnp.float32)).resh...]
    unnamed x15 -> x27, local copies, waits for them, and re-layouts: 2.54 us -> 14.9 us
  transfers between devices with their start and end apart: 11 -> 0, of which waited for: 7 -> 0; matrix products, arithmetic and copies ran while one was open for 9% -> 0% of each run, Pallas kernels for 0% -> 0%
where the time goes in v1:
time: 329 us; the launch traced here: 326 us
  Pallas kernels  300 us (91%)
  local copies, waits for them, and re-layouts  17.9 us (5%)
  other arithmetic  7.67 us (2%)
    pallas_call x1, Pallas kernels, collect(): pl.pallas_call(functools.partial(collect_kernel, planes), out_shape=(out,...  154 us
    pallas_call x1, Pallas kernels, spread(): pl.pallas_call(functools.partial(spread_kernel, planes), out_shape=(tiles...  108 us
    pallas_call x1, Pallas kernels, attention(): pl.pallas_call(functools.partial(attention_kernel, ends.shape[0]), out_sh...  37.8 us
    unnamed x27, local copies, waits for them, and re-layouts  14.9 us

profile of v1, /device:TPU:26, one launch (start us, length us, event | category | flops | bytes accessed | tf_op | source)
XLA Modules:
  0.0 326.0 jit_solution(5721492579981334283)
XLA Ops:
  0.6 1.3 reduce-window.9
  2.0 0.7 broadcast_multiply_fusion
  2.7 1.8 convert_multiply_fusion
  4.6 1.8 reshape.54
  6.4 0.0 copy-start
  6.4 0.0 copy-start.8
  6.4 0.0 copy-start.9
  6.4 3.7 %reduce_sum.9 = f32[1024,4]{1,0:T(8,128)} reduce(f32[1024,4,128]{2,1,0:T(4,128)} %reshape.54, f32[]{:T(128)} %constant.7.clone.1), dimensions={2}, to_apply=%region_1.0 | reduce | flops 520192 | bytes 2113540 | tf_op jit(solution)/shard_map/reduce_sum | solution.py:407
  10.1 1.2 copy.11
  11.4 0.0 copy-done
  11.4 0.0 copy-done.8
  11.4 0.0 copy-done.9
  11.4 0.0 copy-start.10
  11.4 1.2 copy-done.10
  12.6 108.2 %spread.1 = (bf16[2,8,512,128]{3,2,1,0:T(8,128)(2,1)S(1)}, bf16[2,8,512,128]{3,2,1,0:T(8,128)(2,1)S(1)}, f32[2,8,2,512]{3,2,1,0:T(2,128)S(1)}, bf16[8,1024,128]{...) custom-call(bf16[1024,512]{1,0:T(8,128)(2,1)S(1)} %copy-done.8, bf16[1024,512]{1,0:T(8,128)(2,1)S(1)} %copy-done, ...), custom_call_target="tpu_custom_call" | custom-call | tf_op jit(solution)/shard_map/spread/pallas_call | solution.py:150
  120.8 0.0 copy-start.4
  120.8 1.3 copy-done.4
  122.2 0.0 copy-start.5
  122.2 1.3 copy-done.5
  123.5 0.0 copy-start.6
  123.5 1.3 copy-done.6
  124.8 0.0 copy-start.7
  124.8 1.3 copy-done.7
  126.2 0.0 copy-start.11
  126.2 0.6 copy-done.11
  126.8 37.8 %attention.1 = (bf16[2,8,512,128]{3,2,1,0:T(8,128)(2,1)}, bf16[8192,128]{1,0:T(8,128)(2,1)}, bf16[8192,128]{1,0:T(8,128)(2,1)}) custom-call(s32[8]{0:T(128)} %bitcast.16, bf16[2,8,512,128]{3,2,1,0:T(8,128)(2,1)} %copy-done.4, bf16[2,8,512,128]{3,2,1,0:T(8,128)(2,1)} %copy-done.5, f32[2,8,2,512]{3,2,1,0:T(2,128)} %copy-done.11, bf16[8192,128]{1,0:T(8,128)(2,1)} %bitcast.13, ...), custom_call_target="tpu_custom_call" | custom-call | tf_op jit(solution)/shard_map/attention/pallas_call | solution.py:245
  164.6 0.0 copy-start.1
  164.6 1.6 copy-done.1
  166.2 0.0 copy-start.2
  166.2 1.6 copy-done.2
  167.8 0.0 copy-start.3
  167.8 1.6 copy-done.3
  169.4 153.7 %collect.1 = (bf16[1024,512]{1,0:T(8,128)(2,1)S(1)}, bf16[1024,512]{1,0:T(8,128)(2,1)S(1)}, bf16[1024,512]{1,0:T(8,128)(2,1)S(1)}) custom-call(bf16[2,8,512,128]{3,2,1,0:T(8,128)(2,1)S(1)} %copy-done.1, bf16[8,1024,128]{2,1,0:T(8,128)(2,1)S(1)} %bitcast.11, bf16[8,1024,128]{2,1,0:T(8,128)(2,1)S(1)} %bitcast.12), custom_call_target="tpu_custom_call" | custom-call | tf_op jit(solution)/shard_map/collect/pallas_call | solution.py:386
  323.1 1.0 copy.15
  324.1 1.0 copy.16
  325.0 1.0 copy.17
  (2 shorter events, 0.1 us)
Async XLA Ops:
  6.4 5.0 %copy-start = (bf16[1024,512]{1,0:T(8,128)(2,1)S(1)}, bf16[1024,512]{1,0:T(8,128)(2,1)}, u32[]{:S(2)}) copy-start(bf16[1024,512]{1,0:T(8,128)(2,1)} %g_ref.1) | copy-start | bytes 3145732
  6.4 5.0 %copy-start.8 = (bf16[1024,512]{1,0:T(8,128)(2,1)S(1)}, bf16[1024,512]{1,0:T(8,128)(2,1)}, u32[]{:S(2)}) copy-start(bf16[1024,512]{1,0:T(8,128)(2,1)} %q_ref.1) | copy-start | bytes 3145732
  6.4 5.0 %copy-start.9 = (bf16[1024,512]{1,0:T(8,128)(2,1)S(1)}, bf16[1024,512]{1,0:T(8,128)(2,1)}, u32[]{:S(2)}) copy-start(bf16[1024,512]{1,0:T(8,128)(2,1)} %k_ref.1) | copy-start | bytes 3145732
  11.4 1.2 copy-start.10
  120.8 1.3 copy-start.4
  122.2 1.3 copy-start.5
  123.5 1.3 copy-start.6
  124.8 1.3 copy-start.7
  126.2 0.6 copy-start.11
  164.6 1.6 copy-start.1
  166.2 1.6 copy-start.2
  167.8 1.6 copy-start.3

commit v2 on v1

--- a/solution.py
+++ b/solution.py
@@ -14,7 +14,7 @@
 SCALING = HEAD_DIM ** (-0.5)
 LOG2E = math.log2(math.e)
 MESH = pl.DeviceIdType.MESH
-TILE_K = 512
+TILE_K = 1024
 
 
 def dot(a, b, dims):
@@ -22,8 +22,8 @@
 
 
 def spread_kernel(
-    planes, q_ref, g_ref, nd_ref, k_ref, v_ref, qo, go, ndo, ko, vo,
-    send, recv, relay, kv_send, kv_recv, fwd_send, fwd_recv,
+    planes, q_ref, g_ref, nd_ref, k_ref, v_ref, qo, go, ndo, ko, vo, qs, gs, nds,
+    send, recv, stage_recv, stage_send, kv_send, kv_recv, fwd_send, fwd_recv,
 ):
     row = lax.axis_index("qrow")
     z = lax.axis_index("kcol")
@@ -32,31 +32,68 @@
     tile = q_ref.shape[0] // 2
     heads = KV_HEADS
     partner = s * 2 + 1 - core
-    below = jnp.minimum(jnp.maximum(s - z, 0), 1)
-    plane = s - below
-    slot = core * planes + z
 
     def query_parts(h, half):
         rows = pl.ds(half * tile, tile)
         cols = pl.ds(pl.multiple_of(h * HEAD_DIM, HEAD_DIM), HEAD_DIM)
         return q_ref.at[rows, cols], g_ref.at[rows, cols], nd_ref.at[h, half]
 
-    def query_dst(which, j):
-        return qo.at[which, j], go.at[which, j], ndo.at[which, j]
+    def query_dst(j):
+        return qo.at[j], go.at[j], ndo.at[j]
+
+    def staged(src, c0):
+        return qs.at[src, c0], gs.at[src, c0], nds.at[src, c0]
 
     def query_send(i, half, act):
         h = (s + i) % heads
         to = h * 2 + (z + half) % 2
-        home = (to == row) & (plane == z)
-        for t, (a, b) in enumerate(zip(query_parts(h, half), query_dst(below, slot))):
-            there = pltpu.make_async_remote_copy(
-                a, b, send.at[t, i, half], recv.at[t, below, slot],
-                device_id=(to, plane), device_id_type=MESH)
-            if act == "start":
-                pl.when(home)(pltpu.make_async_copy(a, b, recv.at[t, below, slot]).start)
-                pl.when(jnp.logical_not(home))(there.start)
-            else:
-                pl.when(jnp.logical_not(home))(there.wait_send)
+        home = to == row
+        here = s == z
+
+        def move(dst, sem):
+            for t, (a, b) in enumerate(zip(query_parts(h, half), dst)):
+                def remote():
+                    return pltpu.make_async_remote_copy(
+                        a, b, send.at[t, i, half], sem(t),
+                        device_id=(to, z), device_id_type=MESH)
+                if act == "start":
+                    @pl.when(home)
+                    def _():
+                        pltpu.make_async_copy(a, b, sem(t)).start()
+
+                    @pl.when(jnp.logical_not(home))
+                    def _():
+                        remote().start()
+                else:
+                    @pl.when(jnp.logical_not(home))
+                    def _():
+                        remote().wait_send()
+
+        slot = core * planes + z
+
+        @pl.when(here)
+        def _():
+            move(query_dst(slot), lambda t: recv.at[t, slot])
+
+        @pl.when(jnp.logical_not(here))
+        def _():
+            move(staged(s, core), lambda t: stage_recv.at[t, s, core])
+
+    def stage_forward(i, c0, act):
+        src = (s + heads - i) % heads
+        slot = c0 * planes + z
+
+        @pl.when(src != z)
+        def _():
+            for t, (a, b) in enumerate(zip(staged(src, c0), query_dst(slot))):
+                copy = pltpu.make_async_remote_copy(
+                    a, b, stage_send.at[t, src, c0], recv.at[t, slot],
+                    device_id=(row, src), device_id_type=MESH)
+                if act == "start":
+                    pltpu.make_async_copy(a, a, stage_recv.at[t, src, c0]).wait()
+                    copy.start()
+                else:
+                    copy.wait_send()
 
     def key_send(i, act):
         h = (s + i) % heads
@@ -71,24 +108,16 @@
                     device_id=(h * 2 + core, z), device_id_type=MESH)
                 there.start() if act == "start" else there.wait_send()
 
-    def arrived(which, j):
-        for t, b in enumerate(query_dst(which, j)):
-            pltpu.make_async_copy(b, b, recv.at[t, which, j]).wait()
-
-    def pass_on(which, j, act):
-        to = z - 1 + 2 * which
-        for t, (a, b) in enumerate(zip(query_dst(which, j), query_dst(1 - which, j))):
-            copy = pltpu.make_async_remote_copy(
-                a, b, relay.at[t, which, j], recv.at[t, 1 - which, j],
-                device_id=(row, to), device_id_type=MESH)
-            copy.start() if act == "start" else copy.wait_send()
+    def arrived(j):
+        for t, b in enumerate(query_dst(j)):
+            pltpu.make_async_copy(b, b, recv.at[t, j]).wait()
 
     def key_forward(i, act):
-        src = (s + i) % heads
+        src = (s + heads - i) % heads
         for t, b in enumerate((ko, vo)):
             at = b.at[src * 2 + core]
             copy = pltpu.make_async_remote_copy(
-                at, at, fwd_send.at[t, i], fwd_recv.at[t, src],
+                at, at, fwd_send.at[t, src], fwd_recv.at[t, src],
                 device_id=(partner, z), device_id_type=MESH)
             if act == "start":
                 pltpu.make_async_copy(at, at, kv_recv.at[t, src]).wait()
@@ -101,42 +130,22 @@
     for i in range(heads):
         for half in range(2):
             query_send(i, half, "start")
+    for i in range(heads):
         key_send(i, "start")
-
-    def direct(j, z0, act):
-        @pl.when((z0 >= z))
-        def _():
-            if act == "start":
-                arrived(0, j)
-
-            @pl.when(z >= 1)
-            def _():
-                pass_on(0, j, act)
-
-        @pl.when((z0 <= z) & (z + 1 < planes))
-        def _():
-            if act == "start":
-                arrived(1, j)
-            pass_on(1, j, act)
-
-    for z0 in range(planes):
+    for i in range(heads):
         for c0 in range(2):
-            direct(c0 * planes + z0, z0, "start")
+            stage_forward(i, c0, "start")
     for i in range(heads):
         key_forward(i, "start")
-    for z0 in range(planes):
-        for c0 in range(2):
-            j = c0 * planes + z0
-            pl.when(z0 < z)(functools.partial(arrived, 0, j))
-            pl.when((z0 > z) & (z + 1 < planes))(functools.partial(arrived, 1, j))
+    for j in range(2 * planes):
+        arrived(j)
     for i in range(heads):
         for half in range(2):
             query_send(i, half, "wait")
         key_send(i, "wait")
         key_forward(i, "wait")
-    for z0 in range(planes):
         for c0 in range(2):
-            direct(c0 * planes + z0, z0, "wait")
+            stage_forward(i, c0, "wait")
 
 
 def spread(planes, q, g, nd, k, v):
@@ -145,15 +154,18 @@
     anywhere = pl.BlockSpec(memory_space=pl.ANY)
     whole = pl.BlockSpec(memory_space=pltpu.VMEM)
     dma = pltpu.SemaphoreType.DMA
-    tiles = jax.ShapeDtypeStruct((2, slots, n // 2, HEAD_DIM), jnp.bfloat16)
+    tiles = jax.ShapeDtypeStruct((slots, n // 2, HEAD_DIM), jnp.bfloat16)
     keys = jax.ShapeDtypeStruct((2 * KV_HEADS, n, HEAD_DIM), jnp.bfloat16)
+    stage = pltpu.VMEM((KV_HEADS, 2, n // 2, HEAD_DIM), jnp.bfloat16)
     return pl.pallas_call(
         functools.partial(spread_kernel, planes),
-        out_shape=(tiles, tiles, jax.ShapeDtypeStruct((2, slots, 2, n // 2), jnp.float32), keys, keys),
+        out_shape=(tiles, tiles, jax.ShapeDtypeStruct((slots, 2, n // 2), jnp.float32), keys, keys),
         in_specs=[anywhere] * 5,
         out_specs=(whole,) * 5,
         scratch_shapes=[
-            dma((3, KV_HEADS, 2)), dma((3, 2, slots)), dma((3, 2, slots)),
+            stage, stage, pltpu.VMEM((KV_HEADS, 2, 2, n // 2), jnp.float32),
+            dma((3, KV_HEADS, 2)), dma((3, slots)),
+            dma((3, KV_HEADS, 2)), dma((3, KV_HEADS, 2)),
             dma((2, KV_HEADS)), dma((2, KV_HEADS)), dma((2, KV_HEADS)), dma((2, KV_HEADS)),
         ],
         compiler_params=pltpu.CompilerParams(
@@ -163,10 +175,10 @@
 
 
 def attention_kernel(
-    docs, ends_ref, q_ref, g_ref, nd_ref, k_ref, v_ref, dq_ref, dk_ref, dv_ref,
-    dq_acc, dk_acc, dv_acc,
+    which, docs, ends_ref, q_ref, g_ref, nd_ref, k_ref, v_ref, *refs,
 ):
-    slots, tile_q = q_ref.shape[1], q_ref.shape[2]
+    before, (dq_ref, dk_ref, dv_ref, dq_acc, dk_acc, dv_acc) = refs[:-6], refs[-6:]
+    slots, tile_q = q_ref.shape[0], q_ref.shape[1]
     segment = dk_acc.shape[0]
     tile_k = dk_tile = min(TILE_K, segment)
     core = lax.axis_index("qrow") % 2
@@ -178,12 +190,10 @@
             start = jnp.where(position >= ends_ref[d], ends_ref[d], start)
         return start
 
-    dk_acc[...] = jnp.zeros_like(dk_acc)
-    dv_acc[...] = jnp.zeros_like(dv_acc)
-
-    def query_step(i, carry):
-        which = i // slots
-        j = i % slots
+    for i, acc in enumerate((dk_acc, dv_acc)):
+        acc[...] = before[i][...].astype(jnp.float32) if before else jnp.zeros_like(acc)
+
+    def query_step(j, carry):
         q_lo = which * segment + (2 * j + (core + j) % 2) * tile_q
         q_pos = q_lo + lax.broadcasted_iota(jnp.int32, (1, tile_q), 1)
         q_start = doc_start(q_pos + base) - base
@@ -194,9 +204,9 @@
         last = (hi + tile_k - 1) // tile_k
         full_lo = jnp.minimum((last_start + tile_k - 1) // tile_k, last)
         full_hi = jnp.maximum(jnp.minimum((q_lo + 1) // tile_k, last), full_lo)
-        q = q_ref[which, j]
-        g = g_ref[which, j]
-        nd = nd_ref[which, j]
+        q = q_ref[j]
+        g = g_ref[j]
+        nd = nd_ref[j]
         norm = nd[0:1, :]
         delta = nd[1:2, :]
         dq_acc[...] = jnp.zeros_like(dq_acc)
@@ -223,33 +233,33 @@
             lax.fori_loop(full_lo, full_hi, functools.partial(key_step, False), 0)
             lax.fori_loop(full_hi, last, functools.partial(key_step, True), 0)
 
-        dq_ref[which, j] = (dq_acc[...] * SCALING).T.astype(jnp.bfloat16)
+        dq_ref[j] = (dq_acc[...] * SCALING).T.astype(jnp.bfloat16)
         return carry
 
-    lax.fori_loop(0, 2 * slots, query_step, 0)
+    lax.fori_loop(0, slots, query_step, 0)
 
     def finish(kt, carry):
         rows = pl.ds(pl.multiple_of(kt * tile_k, tile_k), tile_k)
-        dk_ref[rows, :] = (dk_acc[rows, :] * SCALING).astype(jnp.bfloat16)
+        dk_ref[rows, :] = (dk_acc[rows, :] * (SCALING if before else 1.0)).astype(jnp.bfloat16)
         dv_ref[rows, :] = dv_acc[rows, :].astype(jnp.bfloat16)
         return carry
 
     lax.fori_loop(0, segment // tile_k, finish, 0)
 
 
-def attention(ends, q, g, nd, k, v):
-    tile_q = q.shape[2]
+def attention(which, ends, q, g, nd, k, v, *before):
+    slots, tile_q = q.shape[:2]
     segment = k.shape[0]
     whole = pl.BlockSpec(memory_space=pltpu.VMEM)
     scalars = pl.BlockSpec(memory_space=pltpu.SMEM)
     return pl.pallas_call(
-        functools.partial(attention_kernel, ends.shape[0]),
+        functools.partial(attention_kernel, which, ends.shape[0]),
         out_shape=(
             jax.ShapeDtypeStruct(q.shape, jnp.bfloat16),
             jax.ShapeDtypeStruct(k.shape, jnp.bfloat16),
             jax.ShapeDtypeStruct(v.shape, jnp.bfloat16),
         ),
-        in_specs=[scalars] + [whole] * 5,
+        in_specs=[scalars] + [whole] * (5 + len(before)),
         out_specs=(whole,) * 3,
         scratch_shapes=[
             pltpu.VMEM((HEAD_DIM, tile_q), jnp.float32),
@@ -257,12 +267,14 @@
             pltpu.VMEM((segment, HEAD_DIM), jnp.float32),
         ],
         compiler_params=pltpu.CompilerParams(vmem_limit_bytes=58 * 1024 * 1024),
-        name="attention",
-    )(ends, q, g, nd, k, v)
+        cost_estimate=pl.CostEstimate(
+            flops=5 * slots * tile_q * segment * HEAD_DIM, bytes_accessed=0, transcendentals=0),
+        name=("attention_own", "attention_next")[which],
+    )(ends, q, g, nd, k, v, *before)
 
 
 def collect_kernel(
-    planes, dq_ref, dk_ref, dv_ref, dqo, dko, dvo, parts, pair, summed,
+    planes, dq_own, dq_next, dk_ref, dv_ref, dqo, dko, dvo, parts, pair, summed,
     send, recv, pair_send, pair_recv, kv_send, kv_recv,
 ):
     row = lax.axis_index("qrow")
@@ -270,7 +282,7 @@
     s = row // 2
     core = row % 2
     heads = KV_HEADS
-    tile = dq_ref.shape[2]
+    tile = dq_own.shape[1]
     n = dko.shape[0]
     partner = s * 2 + 1 - core
     mine = pl.ds(pl.multiple_of(s * HEAD_DIM, HEAD_DIM), HEAD_DIM)
@@ -287,10 +299,11 @@
     def query_return(which, c0, z0, act):
         j = c0 * planes + z0
         half = (core + z0) % 2
+        dq_ref = (dq_own, dq_next)[which]
         to = (z + which) * 2 + c0
         home = (to == row) & (z0 == z)
         copy = pltpu.make_async_remote_copy(
-            dq_ref.at[which, j], parts.at[which, s, half],
+            dq_ref.at[j], parts.at[which, s, half],
             send.at[which, j], recv.at[which, s, half],
             device_id=(to, z0), device_id_type=MESH)
 
@@ -298,7 +311,7 @@
             if act == "start":
                 @pl.when(home)
                 def _():
-                    parts[which, s, half] = dq_ref[which, j]
+                    parts[which, s, half] = dq_ref[j]
                 pl.when(jnp.logical_not(home))(copy.start)
             else:
                 pl.when(jnp.logical_not(home))(copy.wait_send)
@@ -377,8 +390,8 @@
             pltpu.make_async_copy(got, got, kv_recv.at[t, src]).wait()
 
 
-def collect(planes, dq, dk, dv):
-    tile = dq.shape[2]
+def collect(planes, dq, dq_next, dk, dv):
+    tile = dq.shape[1]
     n = dk.shape[1]
     whole = pl.BlockSpec(memory_space=pltpu.VMEM)
     dma = pltpu.SemaphoreType.DMA
@@ -386,7 +399,7 @@
     return pl.pallas_call(
         functools.partial(collect_kernel, planes),
         out_shape=(out,) * 3,
-        in_specs=[whole] * 3,
+        in_specs=[whole] * 4,
         out_specs=(whole,) * 3,
         scratch_shapes=[
             pltpu.VMEM((2, KV_HEADS, 2, tile, HEAD_DIM), jnp.bfloat16),
@@ -398,7 +411,7 @@
         compiler_params=pltpu.CompilerParams(
             has_side_effects=True, vmem_limit_bytes=40 * 1024 * 1024),
         name="collect",
-    )(dq, dk, dv)
+    )(dq, dq_next, dk, dv)
 
 
 def by_segment(planes, query_states, key_states, value_states, saved_output, output_grad,
@@ -414,8 +427,12 @@
     nd = nd.reshape(2, 2, n // 2, KV_HEADS).transpose(3, 1, 0, 2)
     q, g, nd, k, v = spread(planes, query_states, output_grad, nd, key_states, value_states)
     ends = jnp.cumsum(doc_lengths)
-    dq, dk, dv = attention(ends, q, g, nd, k.reshape(-1, HEAD_DIM), v.reshape(-1, HEAD_DIM))
-    return collect(planes, dq, dk.reshape(-1, n, HEAD_DIM), dv.reshape(-1, n, HEAD_DIM))
+    k, v = k.reshape(-1, HEAD_DIM), v.reshape(-1, HEAD_DIM)
+    down = [(i + 1, i) for i in range(planes - 1)]
+    shifted = [lax.ppermute(x, "kcol", down) for x in (q, g, nd)]
+    dq, dk, dv = attention(0, ends, q, g, nd, k, v)
+    dq_next, dk, dv = attention(1, ends, *shifted, k, v, dk, dv)
+    return collect(planes, dq, dq_next, dk.reshape(-1, n, HEAD_DIM), dv.reshape(-1, n, HEAD_DIM))
 
 
 DEAL_Q = 512

time: 329 us -> 229 us (0.70); the launches traced: 326 us -> 230 us
  Pallas kernels: 300 us -> 195 us
  starting transfers between devices: 0 us -> 12.5 us
    pallas_call x1, Pallas kernels: 154 us -> 90.5 us  [collect(): pl.pallas_call(functools.partial(collect_kernel, planes), out_shape=(out,...]
    pallas_call x1, Pallas kernels: 108 us -> 57.5 us  [spread(): pl.pallas_call(functools.partial(spread_kernel, planes), out_shape=(tiles...]
    ppermute x0 -> x3, starting transfers between devices: none -> 12.5 us  [by_segment(): shifted = [lax.ppermute(x, 'kcol', down) for x in (q, g, nd)]]
    pallas_call x1 -> x2, Pallas kernels: 37.8 us -> 46.6 us  [attention(): pl.pallas_call(functools.partial(attention_kernel, which, ends.shape[0]),...]
    unnamed x27 -> x35, local copies, waits for them, and re-layouts: 14.9 us -> 12.5 us
  transfers between devices with their start and end apart: 0 -> 3, of which waited for: 0 -> 0; matrix products, arithmetic and copies ran while one was open for 0% -> 0% of each run, Pallas kernels for 0% -> 16%
where the time goes in v2:
time: 229 us; the launch traced here: 230 us
  Pallas kernels  195 us (85%)
  local copies, waits for them, and re-layouts  15.5 us (7%)
  starting transfers between devices  12.5 us (5%)
  other arithmetic  6.32 us (3%)
    pallas_call x1, Pallas kernels, collect(): pl.pallas_call(functools.partial(collect_kernel, planes), out_shape=(out,...  90.5 us
    pallas_call x1, Pallas kernels, spread(): pl.pallas_call(functools.partial(spread_kernel, planes), out_shape=(tiles...  57.5 us
    pallas_call x2, Pallas kernels, attention(): pl.pallas_call(functools.partial(attention_kernel, which, ends.shape[0]),...  46.6 us
    ppermute x3, starting transfers between devices, by_segment(): shifted = [lax.ppermute(x, 'kcol', down) for x in (q, g, nd)]  12.5 us
    unnamed x35, local copies, waits for them, and re-layouts  12.5 us
  transfers between devices with their start and end apart: 3, of which 0 were waited for; matrix products, arithmetic and copies ran while one was open for 0% of the time, Pallas kernels for 16%

profile of v2, /device:TPU:26, one launch (start us, length us, event | category | flops | bytes accessed | tf_op | source)
XLA Modules:
  0.0 229.8 jit_solution(6138727421921690395)
XLA Ops:
  0.6 1.8 convert_multiply_fusion
  2.5 1.8 reshape.54
  4.2 0.0 copy-start.11
  4.2 0.0 copy-start
  4.2 0.0 copy-start.3
  4.2 0.0 copy-start.4
  4.2 3.7 %reduce_sum.9 = f32[1024,4]{1,0:T(8,128)} reduce(f32[1024,4,128]{2,1,0:T(4,128)} %reshape.54, f32[]{:T(128)} %constant.7.clone.1), dimensions={2}, to_apply=%region_1.0 | reduce | flops 520192 | bytes 2113540 | tf_op jit(solution)/shard_map/reduce_sum | solution.py:420
  8.0 1.2 copy.11
  9.2 0.0 copy-done.11
  9.3 0.0 copy-done
  9.3 0.0 copy-done.3
  9.3 0.0 copy-done.4
  9.3 0.0 copy-start.5
  9.3 1.2 copy-done.5
  10.6 0.0 copy-start.15
  10.6 57.5 %spread.1 = (bf16[8,512,128]{2,1,0:T(8,128)(2,1)}, bf16[8,512,128]{2,1,0:T(8,128)(2,1)}, f32[8,2,512]{2,1,0:T(2,128)S(1)}, bf16[8,1024,128]{2,1,0:T(8,128)(2,1)S(1)}, bf16[8,1024,128]{2,1,0:T(8,128)(2,1)S(1)}) custom-call(bf16[1024,512]{1,0:T(8,128)(2,1)S(1)} %copy-done.3, bf16[1024,512]{1,0:T(8,128)(2,1)S(1)} %copy-done, ...), custom_call_target="tpu_custom_call" | custom-call | tf_op jit(solution)/shard_map/spread/pallas_call | solution.py:160
  68.0 0.0 copy-start.8
  68.0 1.3 copy-done.8
  69.4 0.0 copy-start.9
  69.4 1.3 copy-done.9
  70.7 0.0 copy-start.10
  70.7 8.6 %collective-permute-start = (bf16[8,512,128]{2,1,0:T(8,128)(2,1)}, bf16[8,512,128]{2,1,0:T(8,128)(2,1)S(1)}, u32[]{:S(2)}, u32[]{:S(2)}) collective-permute-start(bf16[8,512,128]{2,1,0:T(8,128)(2,1)} %get-tuple-element.14.q_ref), channel_id=1, source_target_pairs={{1,0},{2,1},{3,2},{5,4},{6,5},{7,6},{9,8},{10,9},{11,10},{13,12},{... | collective-permute-start | bytes 3145736 | tf_op jit(solution)/shard_map/ppermute | solution.py:432
  79.3 1.9 collective-permute-start.1
  81.2 2.0 collective-permute-start.2
  83.2 0.0 copy-done.15
  83.3 0.7 reduce-window.9
  84.0 0.0 copy-done.10
  84.0 37.7 %attention_own.1 = (bf16[8,512,128]{2,1,0:T(8,128)(2,1)}, bf16[8192,128]{1,0:T(8,128)(2,1)}, bf16[8192,128]{1,0:T(8,128)(2,1)}) custom-call(s32[8]{0:T(128)} %bitcast.19, bf16[8,512,128]{2,1,0:T(8,128)(2,1)} %get-tuple-element.14.q_ref, bf16[8,512,128]{2,1,0:T(8,128)(2,1)} %get-tuple-element.15.g_ref, f32[8,2,512]{2,1,0:T(2,128)} %copy-done.10, ...), custom_call_target="tpu_custom_call" | custom-call | flops 21474836480 | tf_op jit(solution)/shard_map/attention_own/pallas_call | solution.py:255
  121.7 0.0 collective-permute-done.2.nd_ref
  121.7 0.0 copy-start.14
  121.7 0.0 collective-permute-done.q_ref
  121.7 0.0 copy-start.12
  121.7 0.0 collective-permute-done.1.g_ref
  121.7 0.0 copy-start.13
  121.7 0.6 copy-done.14
  122.3 0.4 copy-done.12
  122.6 0.3 copy-done.13
  123.0 0.0 copy-start.6
  123.0 8.9 %attention_next.1 = (bf16[8,512,128]{2,1,0:T(8,128)(2,1)}, bf16[8192,128]{1,0:T(8,128)(2,1)}, bf16[8192,128]{1,0:T(8,128)(2,1)}) custom-call(s32[8]{0:T(128)} %bitcast.20, bf16[8,512,128]{2,1,0:T(8,128)(2,1)} %copy-done.12, bf16[8,512,128]{2,1,0:T(8,128)(2,1)} %copy-done.13, f32[8,2,512]{2,1,0:T(2,128)} %copy-done.14, bf16[8192,128]{1,0:T(8,128)(2,1)} %bitcast.14, ...), custom_call_target="tpu_custom_call" | custom-call | flops 21474836480 | tf_op jit(solution)/shard_map/attention_next/pallas_call | solution.py:255
  131.9 0.0 copy-done.6
  131.9 1.6 copy-done.1
  133.5 0.0 copy-start.2
  133.5 1.6 copy-done.2
  135.1 1.2 copy-done.7
  136.3 90.5 %collect.1 = (bf16[1024,512]{1,0:T(8,128)(2,1)S(1)}, bf16[1024,512]{1,0:T(8,128)(2,1)S(1)}, bf16[1024,512]{1,0:T(8,128)(2,1)S(1)}) custom-call(bf16[8,512,128]{2,1,0:T(8,128)(2,1)S(1)} %copy-done.6, bf16[8,512,128]{2,1,0:T(8,128)(2,1)S(1)} %copy-done.7, bf16[8,1024,128]{2,1,0:T(8,128)(2,1)S(1)} %bitcast.11, bf16[8,1024,128]{2,1,0:T(8,128)(2,1)S(1)} %bitcast.12), custom_call_target="tpu_custom_call" | custom-call | tf_op jit(solution)/shard_map/collect/pallas_call | solution.py:399
  226.8 1.0 copy.15
  227.8 1.0 copy.16
  228.8 1.0 copy.17
  (5 shorter events, 0.1 us)
Async XLA Ops:
  4.2 5.0 %copy-start.11 = (f32[1024,4]{0,1:T(4,128)S(1)}, f32[1024,4]{0,1:T(4,128)}, u32[]{:S(2)}) copy-start(f32[1024,4]{0,1:T(4,128)} %param.12) | copy-start | bytes 49156
  4.2 5.1 %copy-start = (bf16[1024,512]{1,0:T(8,128)(2,1)S(1)}, bf16[1024,512]{1,0:T(8,128)(2,1)}, u32[]{:S(2)}) copy-start(bf16[1024,512]{1,0:T(8,128)(2,1)} %g_ref.1) | copy-start | bytes 3145732
  4.2 5.1 %copy-start.3 = (bf16[1024,512]{1,0:T(8,128)(2,1)S(1)}, bf16[1024,512]{1,0:T(8,128)(2,1)}, u32[]{:S(2)}) copy-start(bf16[1024,512]{1,0:T(8,128)(2,1)} %q_ref.1) | copy-start | bytes 3145732
  4.2 5.1 %copy-start.4 = (bf16[1024,512]{1,0:T(8,128)(2,1)S(1)}, bf16[1024,512]{1,0:T(8,128)(2,1)}, u32[]{:S(2)}) copy-start(bf16[1024,512]{1,0:T(8,128)(2,1)} %k_ref.1) | copy-start | bytes 3145732
  9.3 1.2 copy-start.5
  10.6 72.7 %copy-start.15 = (s32[8]{0:T(128)S(1)}, s32[8]{0:T(128)}, u32[]{:S(2)}) copy-start(s32[8]{0:T(128)} %param.13) | copy-start | bytes 100
  68.0 1.3 copy-start.8
  69.4 1.3 copy-start.9
  70.7 13.3 %copy-start.10 = (f32[8,2,512]{2,1,0:T(2,128)}, f32[8,2,512]{2,1,0:T(2,128)S(1)}, u32[]{:S(2)}) copy-start(f32[8,2,512]{2,1,0:T(2,128)S(1)} %get-tuple-element.16.nd_ref) | copy-start | bytes 98308
  70.7 51.0 %collective-permute-start = (bf16[8,512,128]{2,1,0:T(8,128)(2,1)}, bf16[8,512,128]{2,1,0:T(8,128)(2,1)S(1)}, u32[]{:S(2)}, u32[]{:S(2)}) collective-permute-start(bf16[8,512,128]{2,1,0:T(8,128)(2,1)} %get-tuple-element.14.q_ref), channel_id=1, source_target_pairs={{1,0},{2,1},{3,2},{5,4},{6,5},{7,6},{9,8},{10,9},{11,10},{13,12},{... | collective-permute-start | bytes 3145736 | tf_op jit(solution)/shard_map/ppermute | solution.py:432
  79.3 42.4 %collective-permute-start.1 = (bf16[8,512,128]{2,1,0:T(8,128)(2,1)}, bf16[8,512,128]{2,1,0:T(8,128)(2,1)S(1)}, u32[]{:S(2)}, u32[]{:S(2)}) collective-permute-start(bf16[8,512,128]{2,1,0:T(8,128)(2,1)} %get-tuple-element.15.g_ref), channel_id=1, source_target_pairs={{1,0},{2,1},{3,2},{5,4},{6,5},{7,6},{9,8},{10,9},{11,10},{13,12},{... | collective-permute-start | bytes 3145736 | tf_op jit(solution)/shard_map/ppermute | solution.py:432
  81.2 40.5 %collective-permute-start.2 = (f32[8,2,512]{2,1,0:T(2,128)S(1)}, f32[8,2,512]{2,1,0:T(2,128)S(1)}, u32[]{:S(2)}, u32[]{:S(2)}) collective-permute-start(f32[8,2,512]{2,1,0:T(2,128)S(1)} %get-tuple-element.16.nd_ref), channel_id=1, source_target_pairs={{1,0},{2,1},{3,2},{5,4},{6,5},{7,6},{9,8},{10,9},{11,10},{13,12},{... | collective-permute-start | bytes 98312 | tf_op jit(solution)/shard_map/ppermute | solution.py:432
  121.7 0.6 copy-start.14
  121.7 1.0 copy-start.12
  121.7 1.3 copy-start.13
  123.0 8.9 %copy-start.6 = (bf16[8,512,128]{2,1,0:T(8,128)(2,1)S(1)}, bf16[8,512,128]{2,1,0:T(8,128)(2,1)}, u32[]{:S(2)}) copy-start(bf16[8,512,128]{2,1,0:T(8,128)(2,1)} %get-tuple-element.19.dq_own) | copy-start | bytes 3145732
  131.9 1.6 copy-start.1
  133.5 1.6 copy-start.2
  135.1 1.2 copy-start.7

commit v3 on v2

--- a/solution.py
+++ b/solution.py
@@ -169,7 +169,7 @@
             dma((2, KV_HEADS)), dma((2, KV_HEADS)), dma((2, KV_HEADS)), dma((2, KV_HEADS)),
         ],
         compiler_params=pltpu.CompilerParams(
-            has_side_effects=True, vmem_limit_bytes=40 * 1024 * 1024),
+            has_side_effects=True, vmem_limit_bytes=28 * 1024 * 1024),
         name="spread",
     )(q, g, nd, k, v)
 
@@ -266,7 +266,7 @@
             pltpu.VMEM((segment, HEAD_DIM), jnp.float32),
             pltpu.VMEM((segment, HEAD_DIM), jnp.float32),
         ],
-        compiler_params=pltpu.CompilerParams(vmem_limit_bytes=58 * 1024 * 1024),
+        compiler_params=pltpu.CompilerParams(vmem_limit_bytes=36 * 1024 * 1024),
         cost_estimate=pl.CostEstimate(
             flops=5 * slots * tile_q * segment * HEAD_DIM, bytes_accessed=0, transcendentals=0),
         name=("attention_own", "attention_next")[which],
@@ -321,10 +321,10 @@
             pl.when(z + 1 < planes)(move)
 
     def every_query(act):
-        for dz in range(planes):
+        for d in sorted(range(planes), key=lambda d: (d == 0, abs(2 * d - planes))):
             for c0 in range(2):
                 for which in range(2):
-                    query_return(which, c0, dz, act)
+                    query_return(which, c0, (z + d) % planes, act)
 
     for i in range(heads):
         trade(i, "start")
@@ -409,7 +409,7 @@
             dma((2, KV_HEADS)), dma((2, KV_HEADS)), dma((2, KV_HEADS)), dma((2, KV_HEADS)),
         ],
         compiler_params=pltpu.CompilerParams(
-            has_side_effects=True, vmem_limit_bytes=40 * 1024 * 1024),
+            has_side_effects=True, vmem_limit_bytes=28 * 1024 * 1024),
         name="collect",
     )(dq, dq_next, dk, dv)
 
@@ -417,14 +417,12 @@
 def by_segment(planes, query_states, key_states, value_states, saved_output, output_grad,
                normalizer, doc_lengths):
     n = query_states.shape[0]
-    row_delta = jnp.sum(
-        (output_grad.astype(jnp.float32) * saved_output.astype(jnp.float32)).reshape(
-            n, KV_HEADS, HEAD_DIM
-        ),
-        axis=2,
-    )
-    nd = jnp.stack([normalizer * LOG2E, row_delta], axis=0)
-    nd = nd.reshape(2, 2, n // 2, KV_HEADS).transpose(3, 1, 0, 2)
+    product = output_grad.astype(jnp.float32) * saved_output.astype(jnp.float32)
+    member = jnp.repeat(jnp.eye(KV_HEADS, dtype=jnp.float32), HEAD_DIM, axis=1)
+    row_delta = lax.dot_general(
+        member, product, (((1,), (1,)), ((), ())), precision=lax.Precision.HIGHEST)
+    nd = jnp.stack([(normalizer * LOG2E).T, row_delta], axis=1)
+    nd = nd.reshape(KV_HEADS, 2, 2, n // 2).transpose(0, 2, 1, 3)
     q, g, nd, k, v = spread(planes, query_states, output_grad, nd, key_states, value_states)
     ends = jnp.cumsum(doc_lengths)
     k, v = k.reshape(-1, HEAD_DIM), v.reshape(-1, HEAD_DIM)

time: 229 us -> 211 us (0.921)
  Pallas kernels: 195 us -> 185 us
  local copies, waits for them, and re-layouts: 15.5 us -> 10.1 us
  other arithmetic: 6.32 us -> 2.16 us
    pallas_call x2, Pallas kernels: 46.6 us -> 38 us  [attention(): pl.pallas_call(functools.partial(attention_kernel, which, ends.shape[0]),...]
    reduce_sum x1 -> x0, other arithmetic: 3.72 us -> none  [by_segment(): jnp.sum((output_grad.astype(jnp.float32) * saved_output.astype(jnp.float3...]
    unnamed x35 -> x27, local copies, waits for them, and re-layouts: 12.5 us -> 10 us
where the time goes in v3:
time: 211 us; the launch traced here: 213 us
  Pallas kernels  185 us (88%)
  starting transfers between devices  12.5 us (6%)
  local copies, waits for them, and re-layouts  10.1 us (5%)
  other arithmetic  2.16 us (1%)
    pallas_call x1, Pallas kernels, collect(): pl.pallas_call(functools.partial(collect_kernel, planes), out_shape=(out,...  90 us
    pallas_call x1, Pallas kernels, spread(): pl.pallas_call(functools.partial(spread_kernel, planes), out_shape=(tiles...  57.4 us
    pallas_call x2, Pallas kernels, attention(): pl.pallas_call(functools.partial(attention_kernel, which, ends.shape[0]),...  38 us
    ppermute x3, starting transfers between devices, by_segment(): shifted = [lax.ppermute(x, 'kcol', down) for x in (q, g, nd)]  12.5 us
    unnamed x27, local copies, waits for them, and re-layouts  10 us
  transfers between devices with their start and end apart: 3, of which 0 were waited for; matrix products, arithmetic and copies ran while one was open for 0% of the time, Pallas kernels for 16%

profile of v3, /device:TPU:26, one launch (start us, length us, event | category | flops | bytes accessed | tf_op | source)
XLA Modules:
  0.0 213.0 jit_solution(15058202505852609870)
XLA Ops:
  0.6 0.1 broadcast_in_dim.3
  0.7 0.0 copy-start.2
  0.7 1.9 convert_multiply_fusion
  2.7 0.0 copy-start.10
  2.7 0.0 copy-start
  2.7 0.0 copy-start.1
  2.7 1.8 convolution_bitcast_fusion
  4.6 0.0 copy-done.10
  4.7 0.0 copy-done.2
  4.7 0.0 copy-done
  4.7 0.0 copy-done.1
  4.7 0.0 copy-start.3
  4.7 1.2 copy-done.3
  5.9 0.0 copy-start.11
  5.9 57.4 %spread.1 = (bf16[8,512,128]{2,1,0:T(8,128)(2,1)}, bf16[8,512,128]{2,1,0:T(8,128)(2,1)}, f32[8,2,512]{2,1,0:T(2,128)S(1)}, bf16[8,1024,128]{2,1,0:T(8,128)(2,1)S(1)}, bf16[8,1024,128]{2,1,0:T(8,128)(2,1)S(1)}) custom-call(bf16[1024,512]{1,0:T(8,128)(2,1)S(1)} %copy-done.1, bf16[1024,512]{1,0:T(8,128)(2,1)S(1)} %copy-done, ...), custom_call_target="tpu_custom_call" | custom-call | tf_op jit(solution)/shard_map/spread/pallas_call | solution.py:160
  63.4 0.0 copy-start.4
  63.4 1.3 copy-done.4
  64.7 0.0 copy-start.7
  64.7 1.3 copy-done.7
  66.0 8.6 %collective-permute-start = (bf16[8,512,128]{2,1,0:T(8,128)(2,1)}, bf16[8,512,128]{2,1,0:T(8,128)(2,1)S(1)}, u32[]{:S(2)}, u32[]{:S(2)}) collective-permute-start(bf16[8,512,128]{2,1,0:T(8,128)(2,1)} %get-tuple-element.14.q_ref), channel_id=1, source_target_pairs={{1,0},{2,1},{3,2},{5,4},{6,5},{7,6},{9,8},{10,9},{11,10},{13,12},{... | collective-permute-start | bytes 3145736 | tf_op jit(solution)/shard_map/ppermute | solution.py:430
  74.6 1.9 collective-permute-start.1
  76.5 2.0 collective-permute-start.2
  78.6 0.0 copy-done.11
  78.6 0.2 reduce-window.9
  78.8 0.0 copy-start.5
  78.8 1.6 copy-done.5
  80.4 0.0 copy-start.8
  80.4 1.6 copy-done.8
  82.0 0.0 copy-start.6
  82.0 0.0 copy-start.9
  82.0 35.1 %attention_own.1 = (bf16[8,512,128]{2,1,0:T(8,128)(2,1)S(1)}, bf16[8192,128]{1,0:T(8,128)(2,1)S(1)}, bf16[8192,128]{1,0:T(8,128)(2,1)S(1)}) custom-call(s32[8]{0:T(128)S(1)} %bitcast.21, bf16[8,512,128]{2,1,0:T(8,128)(2,1)} %get-tuple-element.14.q_ref, bf16[8,512,128]{2,1,0:T(8,128)(2,1)} %get-tuple-element.15.g_ref, ...), custom_call_target="tpu_custom_call" | custom-call | flops 21474836480 | tf_op jit(solution)/shard_map/attention_own/pallas_call | solution.py:255
  117.1 0.0 collective-permute-done.2.nd_ref
  117.1 0.0 collective-permute-done.q_ref
  117.1 0.0 collective-permute-done.1.g_ref
  117.1 0.0 copy-done.6
  117.1 0.0 copy-done.9
  117.1 2.9 %attention_next.1 = (bf16[8,512,128]{2,1,0:T(8,128)(2,1)S(1)}, bf16[8192,128]{1,0:T(8,128)(2,1)S(1)}, bf16[8192,128]{1,0:T(8,128)(2,1)S(1)}) custom-call(s32[8]{0:T(128)S(1)} %bitcast.22, bf16[8,512,128]{2,1,0:T(8,128)(2,1)S(1)} %collective-permute-done.q_ref, bf16[8,512,128]{2,1,0:T(8,128)(2,1)S(1)} %collective-permute-done.1.g_ref, ...), custom_call_target="tpu_custom_call" | custom-call | flops 21474836480 | tf_op jit(solution)/shard_map/attention_next/pallas_call | solution.py:255
  120.1 90.0 %collect.1 = (bf16[1024,512]{1,0:T(8,128)(2,1)S(1)}, bf16[1024,512]{1,0:T(8,128)(2,1)S(1)}, bf16[1024,512]{1,0:T(8,128)(2,1)S(1)}) custom-call(bf16[8,512,128]{2,1,0:T(8,128)(2,1)S(1)} %get-tuple-element.19.dq_own, bf16[8,512,128]{2,1,0:T(8,128)(2,1)S(1)} %get-tuple-element.22.dq_next, bf16[8,1024,128]{2,1,0:T(8,128)(2,1)S(1)} %bitcast.15, ...), custom_call_target="tpu_custom_call" | custom-call | tf_op jit(solution)/shard_map/collect/pallas_call | solution.py:399
  210.0 1.0 copy.15
  211.0 1.0 copy.16
  212.0 1.0 copy.17
  (6 shorter events, 0.1 us)
Async XLA Ops:
  0.7 3.9 %copy-start.2 = (bf16[1024,512]{1,0:T(8,128)(2,1)S(1)}, bf16[1024,512]{1,0:T(8,128)(2,1)}, u32[]{:S(2)}) copy-start(bf16[1024,512]{1,0:T(8,128)(2,1)} %k_ref.1) | copy-start | bytes 3145732
  2.7 1.9 copy-start.10
  2.7 2.0 copy-start
  2.7 2.0 copy-start.1
  4.7 1.2 copy-start.3
  5.9 72.7 %copy-start.11 = (s32[8]{0:T(128)S(1)}, s32[8]{0:T(128)}, u32[]{:S(2)}) copy-start(s32[8]{0:T(128)} %param.13) | copy-start | bytes 100
  63.4 1.3 copy-start.4
  64.7 1.3 copy-start.7
  66.0 51.1 %collective-permute-start = (bf16[8,512,128]{2,1,0:T(8,128)(2,1)}, bf16[8,512,128]{2,1,0:T(8,128)(2,1)S(1)}, u32[]{:S(2)}, u32[]{:S(2)}) collective-permute-start(bf16[8,512,128]{2,1,0:T(8,128)(2,1)} %get-tuple-element.14.q_ref), channel_id=1, source_target_pairs={{1,0},{2,1},{3,2},{5,4},{6,5},{7,6},{9,8},{10,9},{11,10},{13,12},{... | collective-permute-start | bytes 3145736 | tf_op jit(solution)/shard_map/ppermute | solution.py:430
  74.6 42.5 %collective-permute-start.1 = (bf16[8,512,128]{2,1,0:T(8,128)(2,1)}, bf16[8,512,128]{2,1,0:T(8,128)(2,1)S(1)}, u32[]{:S(2)}, u32[]{:S(2)}) collective-permute-start(bf16[8,512,128]{2,1,0:T(8,128)(2,1)} %get-tuple-element.15.g_ref), channel_id=1, source_target_pairs={{1,0},{2,1},{3,2},{5,4},{6,5},{7,6},{9,8},{10,9},{11,10},{13,12},{... | collective-permute-start | bytes 3145736 | tf_op jit(solution)/shard_map/ppermute | solution.py:430
  76.5 40.6 %collective-permute-start.2 = (f32[8,2,512]{2,1,0:T(2,128)S(1)}, f32[8,2,512]{2,1,0:T(2,128)S(1)}, u32[]{:S(2)}, u32[]{:S(2)}) collective-permute-start(f32[8,2,512]{2,1,0:T(2,128)S(1)} %get-tuple-element.16.nd_ref), channel_id=1, source_target_pairs={{1,0},{2,1},{3,2},{5,4},{6,5},{7,6},{9,8},{10,9},{11,10},{13,12},{... | collective-permute-start | bytes 98312 | tf_op jit(solution)/shard_map/ppermute | solution.py:430
  78.8 1.6 copy-start.5
  80.4 1.6 copy-start.8
  82.0 35.2 %copy-start.6 = (bf16[8,1024,128]{2,1,0:T(8,128)(2,1)S(1)}, bf16[8,1024,128]{2,1,0:T(8,128)(2,1)}, u32[]{:S(2)}) copy-start(bf16[8,1024,128]{2,1,0:T(8,128)(2,1)} %copy-done.4) | copy-start | bytes 6291460
  82.0 35.2 %copy-start.9 = (bf16[8,1024,128]{2,1,0:T(8,128)(2,1)S(1)}, bf16[8,1024,128]{2,1,0:T(8,128)(2,1)}, u32[]{:S(2)}) copy-start(bf16[8,1024,128]{2,1,0:T(8,128)(2,1)} %copy-done.7) | copy-start | bytes 6291460
